TPU v7x, 32 devices: a whole 2x2x4 slice. The times are simulated.
32 devices in a mesh: gx: 4 (over y, x), gy: 2 (over core), gz: 4 (over z).
Axes of the slice: x: 2, y: 2, z: 4, core: 2. Of those that a mesh axis runs over, the one named last changes fastest.
Arguments:
- flow_state: float32 [5, 128, 32, 512], P(None, 'gz', 'gy', 'gx'), may hold values from -5 to 120, as said below
- advection: float32 [3, 5], replicated, may hold values from -400 to 400, as said below
- inverse_x: float32 [5, 128, 128], replicated, may hold values from -1 to 1, as said below
- inverse_y: float32 [5, 16, 16], replicated, may hold values from -1 to 1, as said below
- inverse_z: float32 [5, 32, 32], replicated, may hold values from -1 to 1, as said below
- reduced_x: float32 [5, 16, 16], replicated, as said below
- reduced_y: float32 [5, 8, 8], replicated, as said below
- reduced_z: float32 [5, 16, 16], replicated, as said below
Outputs:
- update: float32 [5, 128, 32, 512], P(None, 'gz', 'gy', 'gx')
- rms_norm: float32 [5], replicated
Inputs may be any that keep to these rules, and one draw needn't show every extreme that they name: flow_state[0] (density) lies between 0.5 and 2, and flow_state[4] / density minus half the squared velocity is at least 0.6 in every cell. `advection`: every entry has magnitude between 100 and 400. inverse_x[v] is the inverse of the 128 x 128 matrix with 4 on the diagonal, advection[0, v] / 2 - 2 just above it, -advection[0, v] / 2 - 2 just below it and 0.5 two places off it. inverse_y[v] is the inverse of the 16 x 16 matrix built likewise from advection[1, v]. inverse_z[v] is the inverse of the 32 x 32 matrix built likewise from advection[2, v]. reduced_x[v] is the inverse of I + K, K being the boundary rows and columns of the block inverses times the coupling between blocks, so that S_x equals the exact solution of the banded system along whole x lines with nothing beyond the grid's ends. reduced_y[v] is built likewise for y lines. reduced_z[v] is built likewise for z lines.
All inputs are finite; a program needn't handle non-finite values.
Results may differ from a plain program's by a relative error of at most 0.0002.
Values sent between devices are 32-bit elements.
A program may use at most 64 MiB of HBM per device.

v0:
```python
import functools

import jax
import jax.numpy as jnp
from jax import lax
from jax.experimental import pallas as pl
from jax.experimental.pallas import tpu as pltpu
from jax.sharding import PartitionSpec as P

MESH = pl.DeviceIdType.MESH
HIGHEST = lax.Precision.HIGHEST
gas_ratio = 0.4
courant = 8000.0
damping = 0.0625
fourth_coef = 0.5
AXES = ("gx", "gy", "gz")

NN = (((1,), (0,)), ((), ()))
NT = (((1,), (1,)), ((), ()))
TN = (((0,), (0,)), ((), ()))


def exact_dot(a, b, dims):
    return lax.dot_general(a, b, dims, precision=HIGHEST, preferred_element_type=jnp.float32)


def halves(a):
    high = a.astype(jnp.bfloat16)
    low = (a - high.astype(jnp.float32)).astype(jnp.bfloat16)
    return high, low


def split_dot(a, b, dims):
    def dot(x, y):
        return lax.dot_general(x, y, dims, preferred_element_type=jnp.float32)

    return dot(a[0], b[0]) + (dot(a[0], b[1]) + dot(a[1], b[0]))


def iota(shape, dim):
    return lax.broadcasted_iota(jnp.int32, shape, dim)


def primitives(u):
    inverse = 1.0 / u[0]
    velocity = [u[1] * inverse, u[2] * inverse, u[3] * inverse]
    kinetic = 0.5 * (velocity[0] * velocity[0] + velocity[1] * velocity[1] + velocity[2] * velocity[2])
    internal = jnp.maximum(u[4] * inverse - kinetic, 0.25)
    pressure = gas_ratio * u[0] * internal
    return velocity, internal, pressure


def fluxes(u, direction, values=None):
    velocity, internal, pressure = primitives(u) if values is None else values
    carried = velocity[direction]
    found = [u[1 + direction]]
    for component in range(3):
        moment = u[1 + component] * carried
        if component == direction:
            moment = moment + pressure
        found.append(moment)
    found.append((u[4] + pressure) * carried)
    return found


def coupling(reduced, index, blocks, speed, load):
    inner = jnp.where(index > 0, 1.0, 0.0).astype(jnp.float32)
    outer = jnp.where(index < blocks - 1, 1.0, 0.0).astype(jnp.float32)
    low = jnp.maximum(4 * index - 2, 0)
    high = jnp.minimum(4 * index + 4, 4 * blocks - 2)
    l0 = load(low) * inner
    l1 = load(low + 1) * inner
    f0 = load(high) * outer
    f1 = load(high + 1) * outer
    g0 = fourth_coef * l0 + (-0.5 * speed - 4.0 * fourth_coef) * l1
    g1 = fourth_coef * l1
    h0 = fourth_coef * f0
    h1 = (0.5 * speed - 4.0 * fourth_coef) * f0 + fourth_coef * f1
    return [g0, g1, h0, h1]


def kernel(dims, state, ax, ay, az, rx, sy, sz, ry, rz, adv, out, stats_out,
           uz, uy, hx, res, edge, field, first, xb, yb, zb, stx, sty, stz, khi, klo, azx,
           in_sem, halo_send, halo_recv, xs, xr, ys, yr, zs, zr, ss, sr):
    counts, nv, cz, cy, cx, cells = dims
    gx, gy, gz = counts
    rows = cz * cy
    me = [lax.axis_index(axis) for axis in AXES]

    loads = []
    for v in range(nv):
        copy = pltpu.make_async_copy(state.at[v], uz.at[v, pl.ds(2 * cy, rows)], in_sem.at[v])
        copy.start()
        loads.append(copy)

    barrier = pltpu.get_barrier_semaphore()
    total = 0
    for axis, count, place in zip(AXES, counts, me):
        for k in range(1, count):
            pl.semaphore_signal(barrier, inc=1, device_id={axis: lax.rem(place + k, count)}, device_id_type=MESH)
            total += 1
    for copy in loads:
        copy.wait()
    pl.semaphore_wait(barrier, total)

    def ring(axis, slot, down_src, down_dst, up_src, up_dst):
        count, place = counts[axis], me[axis]
        lower = lax.rem(place + count - 1, count)
        upper = lax.rem(place + 1, count)
        down = pltpu.make_async_remote_copy(
            src_ref=down_src, dst_ref=down_dst, send_sem=halo_send.at[slot], recv_sem=halo_recv.at[slot],
            device_id={AXES[axis]: lower}, device_id_type=MESH)
        up = pltpu.make_async_remote_copy(
            src_ref=up_src, dst_ref=up_dst, send_sem=halo_send.at[slot + 1], recv_sem=halo_recv.at[slot + 1],
            device_id={AXES[axis]: upper}, device_id_type=MESH)
        down.start()
        up.start()
        return [down, up]

    def spread(axis, src, dst, send, recv):
        count, place = counts[axis], me[axis]
        copies = []
        for k in range(1, count):
            copy = pltpu.make_async_remote_copy(
                src_ref=src, dst_ref=dst, send_sem=send(k - 1), recv_sem=recv(k - 1),
                device_id={AXES[axis]: lax.rem(place + k, count)}, device_id_type=MESH)
            copy.start()
            copies.append(copy)
        return copies

    z_halo = ring(2, 4,
                  uz.at[:, pl.ds(2 * cy, 2 * cy)], uz.at[:, pl.ds((cz + 2) * cy, 2 * cy)],
                  uz.at[:, pl.ds(cz * cy, 2 * cy)], uz.at[:, pl.ds(0, 2 * cy)])

    sub8, lane8 = iota((8, cx), 0), iota((8, cx), 1)
    target = jnp.where(sub8 < 2, sub8, cx - 4 + sub8)
    select = jnp.where((sub8 < 4) & (lane8 == target), 1.0, 0.0).astype(jnp.float32)
    for v in range(nv):
        hx[0, v] = exact_dot(select, uz[v, pl.ds(2 * cy, rows), :], NT)
    x_halo = ring(0, 0, hx.at[0], hx.at[1], hx.at[0], hx.at[2])

    for v in range(nv):
        for y in range(cy):
            uy[v, pl.ds((y + 2) * cz, cz), :] = uz[v, pl.ds(2 * cy + y, cz, stride=cy), :]
    y_halo = ring(1, 2,
                  uy.at[:, pl.ds(2 * cz, 2 * cz)], uy.at[:, pl.ds((cy + 2) * cz, 2 * cz)],
                  uy.at[:, pl.ds(cy * cz, 2 * cz)], uy.at[:, pl.ds(0, 2 * cz)])

    spread_z = jnp.where(iota((cz, rows), 1) // cy == iota((cz, rows), 0), 1.0, 0.0).astype(jnp.float32)
    spread_y = jnp.where(lax.rem(iota((cy, rows), 1), cy) == iota((cy, rows), 0), 1.0, 0.0).astype(jnp.float32)
    for v in range(nv):
        azx[...] = exact_dot(az[v], spread_z, NN)
        wide_y = exact_dot(ay[v], spread_y, NN)

        @pl.loop(0, cz)
        def _(z):
            high, low = halves(azx[pl.ds(z, 1), :] * wide_y)
            at = pl.ds(pl.multiple_of(z * cy, cy), cy)
            khi[v, at, :] = high
            klo[v, at, :] = low

    ux = []
    picked = iota((8 * gx, 4 * gx), 0)
    wanted = jnp.where(lax.rem(picked, 8) < 4, (picked // 8) * 4 + lax.rem(picked, 8), -1)
    expand = jnp.where(iota((8 * gx, 4 * gx), 1) == wanted, 1.0, 0.0).astype(jnp.float32)
    sub_m = iota((8, 4 * gx), 0)
    for v in range(nv):
        m = coupling(rx, me[0], gx, adv[0, v], lambda row: rx[v, pl.ds(row, 1), :])
        table = jnp.where(sub_m == 0, m[0], jnp.where(sub_m == 1, m[1], jnp.where(sub_m == 2, m[2],
                          jnp.where(sub_m == 3, m[3], 0.0))))
        columns = exact_dot(select, ax[v], NT)
        ux.append(exact_dot(exact_dot(expand, table, NT), columns, NN))

    def part(u, direction, centre_values=None):
        ahead = fluxes(u[1], direction)
        behind = fluxes(u[-1], direction)
        found = []
        for v in range(nv):
            fourth = u[-2][v] - 4.0 * u[-1][v] + 6.0 * u[0][v] - 4.0 * u[1][v] + u[2][v]
            found.append(-0.5 * (ahead[v] - behind[v]) - damping * fourth)
        return found

    for copy in y_halo:
        copy.wait_recv()

    @pl.loop(0, cy)
    def _(y):
        u = {}
        for off in range(-2, 3):
            at = pl.ds(pl.multiple_of((y + 2 + off) * cz, cz), cz)
            u[off] = [uy[v, at, :] for v in range(nv)]
        found = part(u, 1)
        for v in range(nv):
            res[v, pl.ds(y, cz, stride=cy), :] = found[v]

    for copy in x_halo:
        copy.wait_recv()
    sub_h = iota((8, rows), 0)
    merged = []
    for v in range(nv):
        fill = 1.0 if v == 0 else 0.0
        both = jnp.where(sub_h < 2, hx[1, v], hx[2, v])
        merged.append(jnp.where(sub_h < 4, both, fill))
    halo_flux = fluxes(merged, 0)

    def at_lane(row, lane, value):
        return jnp.where((sub8 == row) & (lane8 == lane), value, 0.0)

    weights = (at_lane(0, cx - 2, -damping) + at_lane(0, cx - 1, 4.0 * damping) + at_lane(1, cx - 1, -damping)
               + at_lane(2, 0, -damping) + at_lane(3, 0, 4.0 * damping) + at_lane(3, 1, -damping)
               + at_lane(4, cx - 1, -0.5) + at_lane(7, 0, 0.5)).astype(jnp.float32)
    for v in range(nv):
        stacked = jnp.where(sub_h < 4, merged[v], pltpu.roll(halo_flux[v], 4, 0))
        edge[v] = exact_dot(stacked, weights, TN)

    for copy in z_halo:
        copy.wait_recv()

    step = 2 * cy
    lane = iota((step, cx), 1)

    def shifted(a, offset):
        moved = pltpu.roll(a, (-offset) % cx, 1)
        inside = lane < cx - offset if offset > 0 else lane >= -offset
        return jnp.where(inside, moved, 0.0)

    def body(i, carry):
        squares, top = carry
        base = pl.multiple_of(i * step, step)
        u = {}
        for off in range(-2, 3):
            at = pl.ds(pl.multiple_of(base + (off + 2) * cy, cy), step)
            u[off] = [uz[v, at, :] for v in range(nv)]
        found = part(u, 2)
        values = primitives(u[0])
        velocity, internal, _ = values
        wave = (jnp.abs(velocity[0]) + jnp.abs(velocity[1]) + jnp.abs(velocity[2])
                + jnp.sqrt(3.0 * 1.4 * gas_ratio * internal))
        top = jnp.maximum(top, wave)
        flux_x = fluxes(u[0], 0, values)
        new_squares = []
        for v in range(nv):
            c = u[0][v]
            fourth = (shifted(c, -2) + shifted(c, 2)) - 4.0 * (shifted(c, -1) + shifted(c, 1)) + 6.0 * c
            along_x = -0.5 * (shifted(flux_x[v], 1) - shifted(flux_x[v], -1)) - damping * fourth
            at = pl.ds(base, step)
            value = res[v, at, :] + found[v] + (along_x + edge[v, at, :])
            res[v, at, :] = value
            new_squares.append(squares[v] + value * value)
        return tuple(new_squares), top

    zero = jnp.zeros((step, cx), jnp.float32)
    squares, top = lax.fori_loop(0, cz // 2, body, ((zero,) * nv, zero))

    x_copies = []
    for v in range(nv):
        parts = halves(res[v])
        across = halves(ax[v])
        xb[v, me[0]] = split_dot(halves(exact_dot(select, ax[v], NN)), parts, NT)
        x_copies.append(spread(0, xb.at[v, me[0]], xb.at[v, me[0]],
                               lambda k: xs.at[v, k], lambda k: xr.at[v, k]))
        first[v] = split_dot(parts, across, NT)

    sub_s = iota((8, cx), 0)
    tile = jnp.where(sub_s == 5, jnp.max(top, axis=0, keepdims=True), 0.0)
    for v in range(nv):
        tile = jnp.where(sub_s == v, jnp.sum(squares[v], axis=0, keepdims=True), tile)
    stx[me[0]] = tile
    stat_copies = [spread(0, stx.at[me[0]], stx.at[me[0]], lambda k: ss.at[0, k], lambda k: sr.at[0, k])]

    def gathered(ref, count):
        result = ref[0]
        for q in range(1, count):
            result = jnp.where(sub_s < nv, result + ref[q], jnp.maximum(result, ref[q]))
        return result

    y_copies = []
    marks_y = (0, 1, cy - 2, cy - 1)
    marks_z = (0, 1, cz - 2, cz - 1)
    for v in range(nv):
        for copy in x_copies[v]:
            copy.wait_recv()
        every = xb[v].reshape(8 * gx, rows)
        solved = first[v] - split_dot(halves(every), halves(ux[v]), TN)
        parts = halves(solved)
        field[v] = split_dot((khi[v], klo[v]), parts, NN)
        for c, mark in enumerate(marks_y):
            yb[v, me[1], pl.ds(c * cz, cz), :] = field[v, pl.ds(mark, cz, stride=cy), :]
        y_copies.append(spread(1, yb.at[v, me[1]], yb.at[v, me[1]],
                               lambda k: ys.at[v, k], lambda k: yr.at[v, k]))

    for copy in stat_copies[0]:
        copy.wait_recv()
    sty[me[1]] = gathered(stx, gx)
    stat_copies.append(spread(1, sty.at[me[1]], sty.at[me[1]], lambda k: ss.at[1, k], lambda k: sr.at[1, k]))

    def combined(reduced, inverse, axis, v, direction, planes, size):
        count = counts[axis]
        sums = [None] * 4
        for j in range(4 * count):
            m = coupling(reduced, me[axis], count, adv[direction, v], lambda row: reduced[v, row, j])
            plane = planes[v, j // 4, pl.ds((j % 4) * size, size), :]
            for c in range(4):
                term = m[c] * plane
                sums[c] = term if sums[c] is None else sums[c] + term
        return sums

    z_copies = []
    for v in range(nv):
        for copy in y_copies[v]:
            copy.wait_recv()
        sums = combined(ry, sy, 1, v, 1, yb, cz)
        for y in range(cy):
            at = pl.ds(y, cz, stride=cy)
            value = field[v, at, :]
            for c, mark in enumerate(marks_y):
                value = value - sy[v, y, mark] * sums[c]
            field[v, at, :] = value
        zb[v, me[2], pl.ds(0, 2 * cy), :] = field[v, pl.ds(0, 2 * cy), :]
        zb[v, me[2], pl.ds(2 * cy, 2 * cy), :] = field[v, pl.ds((cz - 2) * cy, 2 * cy), :]
        z_copies.append(spread(2, zb.at[v, me[2]], zb.at[v, me[2]],
                               lambda k: zs.at[v, k], lambda k: zr.at[v, k]))
        if v == 0:
            for copy in stat_copies[1]:
                copy.wait_recv()
            stz[me[2]] = gathered(sty, gy)
            stat_copies.append(spread(2, stz.at[me[2]], stz.at[me[2]],
                                      lambda k: ss.at[2, k], lambda k: sr.at[2, k]))

    for copy in stat_copies[2]:
        copy.wait_recv()
    final = gathered(stz, gz)
    norm = jnp.sqrt(jnp.sum(final, axis=1, keepdims=True) / float(cells))
    fastest = courant / jnp.max(final, axis=1, keepdims=True)
    stats_out[...] = jnp.where(sub_s < nv, norm, fastest)
    for v in range(nv):
        for copy in z_copies[v]:
            copy.wait_recv()
        sums = combined(rz, sz, 2, v, 2, zb, cy)
        for z in range(cz):
            value = field[v, pl.ds(z * cy, cy), :]
            for c, mark in enumerate(marks_z):
                value = value - sz[v, z, mark] * sums[c]
            out[v, pl.ds(z * cy, cy), :] = value

    for group in [x_halo, y_halo, z_halo] + x_copies + y_copies + z_copies + stat_copies:
        for copy in group:
            copy.wait_send()


def shards(counts, flow_state, advection, inverse_x, inverse_y, inverse_z, reduced_x, reduced_y, reduced_z):
    nv, cz, cy, cx = flow_state.shape
    gx, gy, gz = counts
    rows = cz * cy
    cells = rows * cx * gx * gy * gz
    most = max(counts) - 1
    vmem = pl.BlockSpec(memory_space=pltpu.VMEM)
    smem = pl.BlockSpec(memory_space=pltpu.SMEM)
    f32 = jnp.float32
    dma = pltpu.SemaphoreType.DMA
    out, stats = pl.pallas_call(
        functools.partial(kernel, (counts, nv, cz, cy, cx, cells)),
        out_shape=(jax.ShapeDtypeStruct((nv, rows, cx), f32), jax.ShapeDtypeStruct((8, cx), f32)),
        in_specs=[pl.BlockSpec(memory_space=pl.ANY), vmem, vmem, vmem, vmem, smem, smem, smem, smem, smem],
        out_specs=(vmem, vmem),
        scratch_shapes=[
            pltpu.VMEM((nv, (cz + 4) * cy, cx), f32),
            pltpu.VMEM((nv, (cy + 4) * cz, cx), f32),
            pltpu.VMEM((3, nv, 8, rows), f32),
            pltpu.VMEM((nv, rows, cx), f32),
            pltpu.VMEM((nv, rows, cx), f32),
            pltpu.VMEM((nv, rows, cx), f32),
            pltpu.VMEM((nv, rows, cx), f32),
            pltpu.VMEM((nv, gx, 8, rows), f32),
            pltpu.VMEM((nv, gy, 4 * cz, cx), f32),
            pltpu.VMEM((nv, gz, 4 * cy, cx), f32),
            pltpu.VMEM((gx, 8, cx), f32),
            pltpu.VMEM((gy, 8, cx), f32),
            pltpu.VMEM((gz, 8, cx), f32),
            pltpu.VMEM((nv, rows, rows), jnp.bfloat16),
            pltpu.VMEM((nv, rows, rows), jnp.bfloat16),
            pltpu.VMEM((cz, rows), f32),
            dma((nv,)),
            dma((6,)), dma((6,)),
            dma((nv, gx - 1)), dma((nv, gx - 1)),
            dma((nv, gy - 1)), dma((nv, gy - 1)),
            dma((nv, gz - 1)), dma((nv, gz - 1)),
            dma((3, most)), dma((3, most)),
        ],
        compiler_params=pltpu.CompilerParams(
            collective_id=0, has_side_effects=True, vmem_limit_bytes=60 * 1024 * 1024),
    )(flow_state.reshape(nv, rows, cx), inverse_x, inverse_y, inverse_z, reduced_x, inverse_y, inverse_z,
      reduced_y, reduced_z, advection)
    update = (out * stats[5, 0]).reshape(flow_state.shape)
    return update, stats[:nv, 0]


def solution(mesh):
    counts = tuple(mesh.shape[axis] for axis in AXES)
    placed = (P(None, "gz", "gy", "gx"), P(), P(), P(), P(), P(), P(), P())
    return jax.shard_map(
        functools.partial(shards, counts),
        mesh=mesh,
        in_specs=placed,
        out_specs=(P(None, "gz", "gy", "gx"), P()),
        check_vma=False,
    )
```

profile of v0, /device:TPU:0, one launch (start us, length us, event | category | flops | bytes accessed | tf_op | source)
XLA Modules:
  0.0 54.7 jit_solution(15399234475119421950)
XLA Ops:
  0.6 49.2 %shard_map.95 = (f32[5,512,128]{2,1,0:T(8,128)}, f32[8,128]{1,0:T(8,128)}) custom-call(f32[5,512,128]{2,1,0:T(8,128)} %bitcast.3, f32[5,128,128]{2,1,0:T(8,128)} %ax.1, f32[5,16,16]{2,1,0:T(8,128)} %sy.1, f32[5,32,32]{2,1,0:T(8,128)} %sz.1, f32[5,16,16]{2,1,0:T(8,128)} %rx.1, f32[5,16,16]{2,1,0:T(8,128)} %sy.1, f32[5,32,32]{2,1,0:T(8,128)} %sz.1, ...), custom_call_target="tpu_custom_call" | custom-call | tf_op jit(solution)/shard_map/pallas_call | solution.py:361
  49.8 1.2 %slice.6 = f32[1,1]{1,0:T(1,128)} slice(f32[8,128]{1,0:T(8,128)} %get-tuple-element.5), slice={[5:6], [0:1]} | slice | bytes 8 | tf_op jit(solution)/shard_map/slice | solution.py:394
  51.0 0.0 copy-start
  51.0 3.1 %broadcast_multiply_fusion = f32[5,512,128]{2,1,0:T(8,128)} fusion(f32[5,512,128]{2,1,0:T(8,128)} %get-tuple-element.4, f32[]{:T(128)} %bitcast.1), kind=kLoop, calls=%fused_computation | loop fusion | flops 327680 | bytes 2621444 | tf_op jit(solution)/shard_map/mul | solution.py:394
  54.1 0.0 copy-done
  54.1 0.6 %slice_reduce_fusion = f32[5]{0:T(128)} fusion(f32[8,128]{1,0:T(8,128)S(1)} %copy-done), kind=kLoop, calls=%fused_computation.1 | loop fusion | bytes 40 | tf_op jit(solution)/shard_map/slice | solution.py:395
Async XLA Ops:
  51.0 3.1 %copy-start = (f32[8,128]{1,0:T(8,128)S(1)}, f32[8,128]{1,0:T(8,128)}, u32[]{:S(2)}) copy-start(f32[8,128]{1,0:T(8,128)} %get-tuple-element.5) | copy-start | bytes 12292
where the time goes:
time: 55 us; the launch traced here: 54.7 us
  Pallas kernels  49.2 us (89%)
  other arithmetic  3.1 us (6%)
  local copies, waits for them, and re-layouts  1.82 us (3%)
  between operations  0.64 us (1%)
    pallas_call x1, Pallas kernels, shards(): pl.pallas_call(functools.partial(kernel, (counts, nv, cz, cy, cx, cells))...  49.2 us
    mul x1, other arithmetic, shards(): update = (out * stats[5, 0]).reshape(flow_state.shape)  3.1 us
    slice x1, local copies, waits for them, and re-layouts, shards(): update = (out * stats[5, 0]).reshape(flow_state.shape)  1.19 us

commit v1 on v0

v1 whole, which is shorter than its diff:
```python
import functools

import jax
import jax.numpy as jnp
from jax import lax
from jax.experimental import pallas as pl
from jax.experimental.pallas import tpu as pltpu
from jax.sharding import PartitionSpec as P

MESH = pl.DeviceIdType.MESH
HIGHEST = lax.Precision.HIGHEST
gas_ratio = 0.4
courant = 8000.0
damping = 0.0625
fourth_coef = 0.5
AXES = ("gx", "gy", "gz")
f32 = jnp.float32
bf16 = jnp.bfloat16

NN = (((1,), (0,)), ((), ()))
NT = (((1,), (1,)), ((), ()))
TN = (((0,), (0,)), ((), ()))


def exact_dot(a, b, dims=NN):
    return lax.dot_general(a, b, dims, precision=HIGHEST, preferred_element_type=f32)


def one_dot(a, b, dims=NN):
    return lax.dot_general(a, b, dims, preferred_element_type=f32)


def halves(a):
    high = a.astype(bf16)
    low = (a - high.astype(f32)).astype(bf16)
    return high, low


def split_dot(a, b, dims=NN):
    return one_dot(a[0], b[0], dims) + (one_dot(a[0], b[1], dims) + one_dot(a[1], b[0], dims))


def stack3(a):
    high, low = halves(a)
    return jnp.concatenate([high, low, high], axis=0)


def iota(shape, dim):
    return lax.broadcasted_iota(jnp.int32, shape, dim)


def ones_where(mask):
    return jnp.where(mask, 1.0, 0.0).astype(f32)


def primitives(u):
    inverse = 1.0 / u[0]
    velocity = [u[1] * inverse, u[2] * inverse, u[3] * inverse]
    kinetic = 0.5 * (velocity[0] * velocity[0] + velocity[1] * velocity[1] + velocity[2] * velocity[2])
    internal = jnp.maximum(u[4] * inverse - kinetic, 0.25)
    pressure = gas_ratio * u[0] * internal
    return velocity, internal, pressure


def fluxes(u, direction, values=None):
    velocity, internal, pressure = primitives(u) if values is None else values
    carried = velocity[direction]
    found = [u[1 + direction]]
    for component in range(3):
        moment = u[1 + component] * carried
        if component == direction:
            moment = moment + pressure
        found.append(moment)
    found.append((u[4] + pressure) * carried)
    return found


def coupled(col, block, part, speed):
    lower = -0.5 * speed - 4.0 * fourth_coef
    upper = 0.5 * speed - 4.0 * fourth_coef
    value = jnp.where((part == 0) & (col == 4 * block - 2), fourth_coef, 0.0)
    value = jnp.where((part == 0) & (col == 4 * block - 1), lower, value)
    value = jnp.where((part == 1) & (col == 4 * block - 1), fourth_coef, value)
    value = jnp.where((part == 2) & (col == 4 * block + 4), fourth_coef, value)
    value = jnp.where((part == 3) & (col == 4 * block + 4), upper, value)
    return jnp.where((part == 3) & (col == 4 * block + 5), fourth_coef, value).astype(f32)


def face_pick(shape, size, row_dim=0):
    r, c = iota(shape, row_dim), iota(shape, 1 - row_dim)
    return ones_where((r < 4) & (c == jnp.where(r < 2, r, size - 4 + r)))


def kernel(dims, state_h, adv_h, ax_h, ay_h, az_h, rx_h, ry_h, rz_h, out, stats_out,
           uz, uy, hx, res, edge, field, first, ext, wyh, wyl, wts, pts, pto, khi, klo, azx, kue, mb, cxf,
           xb, ysend, yrecv, zsend, zrecv, esend, erecv, stx, sty, stz,
           ax, ay, az, rx, ry, rz, adv,
           in_sem, aux_sem, halo_send, halo_recv, xs, xr, ys, yr, zs, zr, es, er, ss, sr):
    counts, nv, cz, cy, cx, cells = dims
    gx, gy, gz = counts
    rows = cz * cy
    pack = xb.shape[1]
    nc = 2 if gy == 2 else 4
    plane4 = 4 * cy
    me = [lax.axis_index(axis) for axis in AXES]

    loads = []
    for v in range(nv):
        copy = pltpu.make_async_copy(state_h.at[v], uz.at[v, pl.ds(2 * cy, rows)], in_sem.at[v])
        copy.start()
        loads.append(copy)
    aux = []
    for i, (src, dst) in enumerate([(az_h, az), (ay_h, ay), (ry_h, ry), (rz_h, rz), (rx_h, rx), (adv_h, adv), (ax_h, ax)]):
        copy = pltpu.make_async_copy(src, dst, aux_sem.at[i])
        copy.start()
        aux.append(copy)

    barrier = pltpu.get_barrier_semaphore()
    total = 0
    for axis, count, place in zip(AXES, counts, me):
        for k in range(1, count):
            pl.semaphore_signal(barrier, inc=1, device_id={axis: lax.rem(place + k, count)}, device_id_type=MESH)
            total += 1
    for copy in loads:
        copy.wait()

    lane_c = iota((rows, cx), 1)

    def faces_to_rows(load):
        packed = jnp.zeros((rows, cx), f32)
        for v in range(nv):
            moved = pltpu.roll(load(v), 4 * v + 2, 1)
            packed = jnp.where(lane_c // 4 == v, moved, packed)
        return jnp.transpose(packed)[0:pack]

    hx[0] = faces_to_rows(lambda v: uz[v, pl.ds(2 * cy, rows), :])
    pl.semaphore_wait(barrier, total)

    def ring(axis, slot, down_src, down_dst, up_src, up_dst, far_first=False):
        count, place = counts[axis], me[axis]
        lower = lax.rem(place + count - 1, count)
        upper = lax.rem(place + 1, count)
        down = pltpu.make_async_remote_copy(
            src_ref=down_src, dst_ref=down_dst, send_sem=halo_send.at[slot], recv_sem=halo_recv.at[slot],
            device_id={AXES[axis]: lower}, device_id_type=MESH)
        up = pltpu.make_async_remote_copy(
            src_ref=up_src, dst_ref=up_dst, send_sem=halo_send.at[slot + 1], recv_sem=halo_recv.at[slot + 1],
            device_id={AXES[axis]: upper}, device_id_type=MESH)
        if far_first:
            @pl.when(place == count - 1)
            def _():
                up.start()
                down.start()

            @pl.when(place < count - 1)
            def _():
                down.start()
                up.start()
        else:
            down.start()
            up.start()
        return [down, up]

    def spread(axis, src, dst, send, recv):
        count, place = counts[axis], me[axis]
        copies = []
        for k in range(1, count):
            target = lax.rem(place + k, count)
            copy = pltpu.make_async_remote_copy(
                src_ref=src(target), dst_ref=dst, send_sem=send(k - 1), recv_sem=recv(k - 1),
                device_id={AXES[axis]: target}, device_id_type=MESH)
            copy.start()
            copies.append(copy)
        return copies

    z_halo = ring(2, 4,
                  uz.at[:, pl.ds(2 * cy, 2 * cy)], uz.at[:, pl.ds((cz + 2) * cy, 2 * cy)],
                  uz.at[:, pl.ds(cz * cy, 2 * cy)], uz.at[:, pl.ds(0, 2 * cy)], far_first=True)
    x_halo = ring(0, 0, hx.at[0], hx.at[1], hx.at[0], hx.at[2])

    for v in range(nv):
        for y in range(cy):
            uy[v, pl.ds((y + 2) * cz, cz), :] = uz[v, pl.ds(2 * cy + y, cz, stride=cy), :]
    y_halo = ring(1, 2,
                  uy.at[:, pl.ds(2 * cz, 2 * cz)], uy.at[:, pl.ds((cy + 2) * cz, 2 * cz)],
                  uy.at[:, pl.ds(cy * cz, 2 * cz)], uy.at[:, pl.ds(0, 2 * cz)])

    for copy in aux:
        copy.wait()

    spread_z = ones_where(iota((cz, rows), 1) // cy == iota((cz, rows), 0))
    spread_y = ones_where(lax.rem(iota((cy, rows), 1), cy) == iota((cy, rows), 0))
    for v in range(nv):
        azx[...] = exact_dot(az[v], spread_z)
        wide_y = exact_dot(ay[v], spread_y)

        @pl.loop(0, cz)
        def _(z):
            high, low = halves(azx[pl.ds(z, 1), :] * wide_y)
            at = pl.ds(pl.multiple_of(z * cy, cy), cy)
            khi[v, at, :] = high
            klo[v, at, :] = low

    nd = wyh.shape[1] // cz
    row_y, col_y = iota((nd, 4 * gy), 0), iota((nd, 4 * gy), 1)
    block_y = row_y // nc
    part_y = row_y % nc + (jnp.where(block_y == 0, 2, 0) if nc == 2 else 0)
    pick_y = iota((4 * gy, 8), 0)
    pick_y = ones_where((pick_y == 4 * me[1] + iota((4 * gy, 8), 1)) & (iota((4 * gy, 8), 1) < 4))
    same_z = iota((cz, rows), 1) // cy == iota((cz, rows), 0)
    for v in range(nv):
        response = exact_dot(exact_dot(ry[v], pick_y), exact_dot(face_pick((8, cy), cy), ay[v]))
        wide = exact_dot(exact_dot(coupled(col_y, block_y, part_y, adv[1, v]), response), spread_y)
        for n in range(nd):
            high, low = halves(jnp.where(same_z, wide[n:n + 1, :], 0.0))
            wyh[v, pl.ds(n * cz, cz), :] = high
            wyl[v, pl.ds(n * cz, cz), :] = low

    nz = wts.shape[1] // cy
    row_z, col_z = iota((nz, 4 * gz), 0), iota((nz, 4 * gz), 1)
    dest = row_z // 2
    wanted = jnp.where(dest > me[2], 4 * dest - 2, 4 * dest + 4) + row_z % 2
    sel_z = ones_where((dest != me[2]) & (col_z == wanted) & (dest < gz))
    pick_z = ones_where((iota((4 * gz, 8), 0) == 4 * me[2] + iota((4 * gz, 8), 1)) & (iota((4 * gz, 8), 1) < 4))
    width = wts.shape[2]
    tiled = ones_where(lax.rem(iota((8, width), 1), plane4) // cy == iota((8, width), 0))
    low_lane = iota((1, width), 1) >= 2 * plane4
    same_y = lax.rem(iota((cy, width), 1), cy) == iota((cy, width), 0)

    def stacked(a):
        high = a.astype(bf16).astype(f32)
        return jnp.where(low_lane, a - high, high)

    for v in range(nv):
        given = stacked(exact_dot(exact_dot(sel_z, exact_dot(rz[v], pick_z)), tiled))
        for n in range(nz):
            wts[v, pl.ds(n * cy, cy), :] = jnp.where(same_y, given[n:n + 1, :], 0.0).astype(bf16)

    def part(u, direction):
        ahead = fluxes(u[1], direction)
        behind = fluxes(u[-1], direction)
        found = []
        for v in range(nv):
            fourth = u[-2][v] - 4.0 * u[-1][v] + 6.0 * u[0][v] - 4.0 * u[1][v] + u[2][v]
            found.append(-0.5 * (ahead[v] - behind[v]) - damping * fourth)
        return found

    for copy in y_halo:
        copy.wait_recv()

    @pl.loop(0, cy)
    def _(y):
        u = {}
        for off in range(-2, 3):
            at = pl.ds(pl.multiple_of((y + 2 + off) * cz, cz), cz)
            u[off] = [uy[v, at, :] for v in range(nv)]
        found = part(u, 1)
        for v in range(nv):
            res[v, pl.ds(y, cz, stride=cy), :] = found[v]

    for copy in x_halo:
        copy.wait_recv()
    sub4 = iota((4, rows), 0)
    merged = [jnp.where(sub4 < 2, hx[2, 4 * v:4 * v + 4, :], hx[1, 4 * v:4 * v + 4, :]) for v in range(nv)]
    halo_flux = fluxes(merged, 0)
    sub8, lane8 = iota((8, cx), 0), iota((8, cx), 1)

    def at_lane(row, lane, value):
        return jnp.where((sub8 == row) & (lane8 == lane), value, 0.0)

    weights = (at_lane(0, 0, -damping) + at_lane(1, 0, 4.0 * damping) + at_lane(1, 1, -damping)
               + at_lane(2, cx - 2, -damping) + at_lane(2, cx - 1, 4.0 * damping) + at_lane(3, cx - 1, -damping)
               + at_lane(6, cx - 1, -0.5) + at_lane(5, 0, 0.5)).astype(bf16)
    weights = jnp.concatenate([weights, weights], axis=0)
    weights = jnp.concatenate([weights, weights], axis=0)
    for v in range(nv):
        both = jnp.concatenate([merged[v], halo_flux[v]], axis=0)
        high = both.astype(bf16).astype(f32)
        mid = (both - high).astype(bf16).astype(f32)
        parts = jnp.concatenate([high, mid, both - high - mid, jnp.zeros_like(both)], axis=0).astype(bf16)
        edge[v] = one_dot(parts, weights, TN)

    step = 2 * cy
    lane = iota((step, cx), 1)

    def shifted(a, offset):
        moved = pltpu.roll(a, (-offset) % cx, 1)
        inside = lane < cx - offset if offset > 0 else lane >= -offset
        return jnp.where(inside, moved, 0.0)

    def body(i, carry):
        squares, top = carry
        base = pl.multiple_of(i * step, step)
        u = {}
        for off in range(-2, 3):
            at = pl.ds(pl.multiple_of(base + (off + 2) * cy, cy), step)
            u[off] = [uz[v, at, :] for v in range(nv)]
        found = part(u, 2)
        values = primitives(u[0])
        velocity, internal, _ = values
        wave = (jnp.abs(velocity[0]) + jnp.abs(velocity[1]) + jnp.abs(velocity[2])
                + jnp.sqrt(3.0 * 1.4 * gas_ratio * internal))
        top = jnp.maximum(top, wave)
        flux_x = fluxes(u[0], 0, values)
        new_squares = []
        for v in range(nv):
            c = u[0][v]
            fourth = (shifted(c, -2) + shifted(c, 2)) - 4.0 * (shifted(c, -1) + shifted(c, 1)) + 6.0 * c
            along_x = -0.5 * (shifted(flux_x[v], 1) - shifted(flux_x[v], -1)) - damping * fourth
            at = pl.ds(base, step)
            value = res[v, at, :] + found[v] + (along_x + edge[v, at, :])
            res[v, at, :] = value
            new_squares.append(squares[v] + value * value)
        return tuple(new_squares), top

    zero = jnp.zeros((step, cx), f32)
    last = cz // 2 - 1
    carry = lax.fori_loop(1, last, body, ((zero,) * nv, zero))
    for copy in z_halo:
        copy.wait_recv()
    squares, top = lax.fori_loop(0, 2, lambda j, c: body(j * last, c), carry)

    y_copies = []
    for v in range(nv):
        inner = split_dot(halves(res[v]), halves(ax[v]), NT)
        first[v] = inner
        ysend[v] = split_dot((wyh[v], wyl[v]), halves(inner))[0:gy * nc * cz].reshape(gy, nc * cz, cx)
        y_copies.append(spread(1, lambda t: ysend.at[v, t], yrecv.at[v, me[1]],
                               lambda k: ys.at[v, k], lambda k: yr.at[v, k]))

    sub_s = iota((8, cx), 0)
    tile = jnp.where(sub_s == 5, jnp.max(top, axis=0, keepdims=True), 0.0)
    for v in range(nv):
        tile = jnp.where(sub_s == v, jnp.sum(squares[v], axis=0, keepdims=True), tile)
    sty[me[1]] = tile
    stat_copies = [spread(1, lambda t: sty.at[me[1]], sty.at[me[1]], lambda k: ss.at[0, k], lambda k: sr.at[0, k])]

    def gathered(ref, count):
        result = ref[0]
        for q in range(1, count):
            result = jnp.where(sub_s < nv, result + ref[q], jnp.maximum(result, ref[q]))
        return result

    def end_planes(ref, v):
        return jnp.concatenate([ref[v, pl.ds(0, 2 * cy), :], ref[v, pl.ds((cz - 2) * cy, 2 * cy), :]], axis=0)

    z_copies = []
    for v in range(nv):
        for copy in y_copies[v]:
            copy.wait_recv()
        taken = ysend[v, me[1]]
        for k in range(1, gy):
            taken = taken + yrecv[v, lax.rem(me[1] + k, gy)]
        start = jnp.where(me[1] == 0, cy - 2, 0)
        for c in range(nc):
            at = pl.ds(start + c, cz, stride=cy) if nc == 2 else pl.ds(c if c < 2 else cy - 4 + c, cz, stride=cy)
            first[v, at, :] = first[v, at, :] - taken[c * cz:(c + 1) * cz]
        field[v] = split_dot((khi[v], klo[v]), halves(first[v]))
        zsend[v] = one_dot(wts[v], stack3(end_planes(field, v)))[0:gz * 2 * cy].reshape(gz, 2 * cy, cx)
        z_copies.append(spread(2, lambda t: zsend.at[v, t], zrecv.at[v, me[2]],
                               lambda k: zs.at[v, k], lambda k: zr.at[v, k]))

    xb[me[0]] = faces_to_rows(lambda v: field[v])
    x_copies = [spread(0, lambda t: xb.at[me[0]], xb.at[me[0]], lambda k: xs.at[k], lambda k: xr.at[k])]
    for copy in stat_copies[0]:
        copy.wait_recv()
    stx[me[0]] = gathered(sty, gy)
    stat_copies.append(spread(0, lambda t: stx.at[me[0]], stx.at[me[0]], lambda k: ss.at[1, k], lambda k: sr.at[1, k]))

    mb[...] = jnp.zeros_like(mb)
    cxf[...] = jnp.zeros_like(cxf)
    wide_x = gx * pack
    in_x = lax.rem(iota((4 * gx, wide_x), 1), pack)
    block_x = iota((4 * gx, wide_x), 1) // pack
    row_x = iota((8, 4 * gx), 0)
    for v in range(nv):
        m = exact_dot(coupled(iota((8, 4 * gx), 1), me[0], row_x, adv[0, v]), rx[v])
        to_pack = ones_where((in_x // 4 == v) & (iota((4 * gx, wide_x), 0) == 4 * block_x + lax.rem(in_x + 2, 4)))
        placed = exact_dot(m, to_pack)
        columns = exact_dot(face_pick((8, cx), cx), ax[v], NT)
        high = columns.astype(bf16).astype(f32)
        for k in range(3):
            at = pl.ds(4 * v + 32 * k, 4)
            mb[at, :] = placed[0:4]
            cxf[at, v * cx:(v + 1) * cx] = (high if k < 2 else columns - high)[0:4]

    row_l, col_l = iota((8, 4 * gz), 0), iota((8, 4 * gz), 1)
    sel_lf = ones_where((row_l < 4) & (col_l == 4 * me[2] + jnp.where(row_l < 2, row_l - 2, row_l + 2)))
    r8, c8 = iota((8, 8), 0), iota((8, 8), 1)
    for v in range(nv):
        near = exact_dot(sel_lf, rz[v])
        square = exact_dot(near, sel_lf, NT)

        def e(i, j):
            return square[i:i + 1, j:j + 1]

        det_l = e(0, 0) * e(1, 1) - e(0, 1) * e(1, 0)
        det_f = e(2, 2) * e(3, 3) - e(2, 3) * e(3, 2)
        inv_l = 1.0 / jnp.where(me[2] > 0, det_l, 1.0)
        inv_f = 1.0 / jnp.where(me[2] < gz - 1, det_f, 1.0)
        mix = ones_where((r8 == c8) & (r8 < 4))
        for i in range(2):
            for j, value in enumerate([(e(2 + i, 0) * e(1, 1) - e(2 + i, 1) * e(1, 0)) * inv_l,
                                       (e(2 + i, 1) * e(0, 0) - e(2 + i, 0) * e(0, 1)) * inv_l]):
                mix = jnp.where((r8 == 2 + i) & (c8 == j), value, mix)
            for j, value in enumerate([(e(i, 2) * e(3, 3) - e(i, 3) * e(3, 2)) * inv_f,
                                       (e(i, 3) * e(2, 2) - e(i, 2) * e(2, 3)) * inv_f]):
                mix = jnp.where((r8 == i) & (c8 == 2 + j), value, mix)
        speed = adv[2, v]
        weigh = jnp.where((r8 == c8) & (r8 < 4), fourth_coef, 0.0)
        weigh = jnp.where((r8 == 0) & (c8 == 1), -0.5 * speed - 4.0 * fourth_coef, weigh)
        weigh = jnp.where((r8 == 3) & (c8 == 2), 0.5 * speed - 4.0 * fourth_coef, weigh).astype(f32)
        columns = exact_dot(az[v], face_pick((8, cz), cz), NT)
        peers = exact_dot(weigh, mix)
        own = exact_dot(weigh, exact_dot(near, pick_z))
        kue[v, 0] = stacked(exact_dot(exact_dot(columns, peers), tiled))
        kue[v, 1] = stacked(exact_dot(exact_dot(columns, own), tiled))

    @pl.loop(0, cz)
    def _(z):
        at = pl.ds(pl.multiple_of(z * cy, cy), cy)
        for v in range(nv):
            pts[v, at, :] = jnp.where(same_y, kue[v, 0, pl.ds(z, 1), :], 0.0).astype(bf16)
            pto[v, at, :] = jnp.where(same_y, kue[v, 1, pl.ds(z, 1), :], 0.0).astype(bf16)

    for v in range(nv):
        field[v] = field[v] - one_dot(pto[v], stack3(end_planes(field, v)))

    for group in x_copies + [stat_copies[1]]:
        for copy in group:
            copy.wait_recv()
    stz[me[2]] = gathered(stx, gx)
    stat_copies.append(spread(2, lambda t: stz.at[me[2]], stz.at[me[2]], lambda k: ss.at[2, k], lambda k: sr.at[2, k]))

    ext[...] = jnp.transpose(split_dot(halves(mb[...]), halves(xb[...].reshape(wide_x, rows))))
    lane_e = iota((plane4, cx), 1)
    lane_v = jnp.where(lane_e < 96, (lane_e % 32) // 4, -1)
    ends = jnp.concatenate([ext[pl.ds(0, 2 * cy), :], ext[pl.ds((cz - 2) * cy, 2 * cy), :]], axis=0)

    def by_variable(table, a):
        result = None
        for v in range(nv):
            term = one_dot(table[v], stack3(jnp.where(lane_v == v, a, 0.0)))
            result = term if result is None else result + term
        return result

    esend[...] = by_variable(wts, ends)[0:gz * 2 * cy].reshape(gz, 2 * cy, cx)
    e_copies = spread(2, lambda t: esend.at[t], erecv.at[me[2]], lambda k: es.at[k], lambda k: er.at[k])
    ext[...] = ext[...] - by_variable(pto, ends)

    def sides(load):
        before, after = None, None
        for k in range(1, gz):
            q = lax.rem(me[2] + k, gz)
            value = load(q)
            left, right = jnp.where(q < me[2], value, 0.0), jnp.where(q > me[2], value, 0.0)
            before = left if before is None else before + left
            after = right if after is None else after + right
        return jnp.concatenate([before, after], axis=0)

    for v in range(nv):
        for copy in z_copies[v]:
            copy.wait_recv()
        field[v] = field[v] - one_dot(pts[v], stack3(sides(lambda q: zrecv[v, q])))

    for copy in stat_copies[2]:
        copy.wait_recv()
    final = gathered(stz, gz)
    norm = jnp.sqrt(jnp.sum(final, axis=1, keepdims=True) / float(cells))
    fastest = courant / jnp.max(final, axis=1, keepdims=True)
    stats_out[...] = jnp.broadcast_to(norm, (8, cx))
    time_step = fastest[5:6, :]

    for copy in e_copies:
        copy.wait_recv()
    solved = ext[...] - by_variable(pts, sides(lambda q: erecv[q]))
    high = solved.astype(bf16).astype(f32)
    parts = jnp.where((lane_c >= 32) & (lane_c < 64), solved - high, high).astype(bf16)
    for v in range(nv):
        out[v] = (field[v] - one_dot(parts, cxf[:, v * cx:(v + 1) * cx].astype(bf16))) * time_step

    for group in [x_halo, y_halo, z_halo, e_copies] + x_copies + y_copies + z_copies + stat_copies:
        for copy in group:
            copy.wait_send()


def finish(nv, solved, stats, update, norm, sem):
    copies = []
    for v in range(nv):
        copy = pltpu.make_async_copy(solved.at[v], update.at[v], sem.at[v])
        copy.start()
        copies.append(copy)
    for v in range(nv):
        norm[v] = stats[v, 0]
    for copy in copies:
        copy.wait()


def shards(counts, flow_state, advection, inverse_x, inverse_y, inverse_z, reduced_x, reduced_y, reduced_z):
    nv, cz, cy, cx = flow_state.shape
    gx, gy, gz = counts
    rows = cz * cy
    cells = rows * cx * gx * gy * gz
    most = max(counts) - 1
    hbm = pl.BlockSpec(memory_space=pltpu.HBM)
    vmem = pl.BlockSpec(memory_space=pltpu.VMEM)
    dma = pltpu.SemaphoreType.DMA
    pack = -(-4 * nv // 8) * 8
    nc = 2 if gy == 2 else 4
    nd = max(8, gy * nc)
    nz = max(8, 2 * gz)
    width = 12 * cy
    out, stats = pl.pallas_call(
        functools.partial(kernel, (counts, nv, cz, cy, cx, cells)),
        out_shape=(pltpu.VMEM((nv, rows, cx), f32), pltpu.VMEM((8, cx), f32)),
        in_specs=[hbm] * 8,
        out_specs=(vmem, vmem),
        scratch_shapes=[
            pltpu.VMEM((nv, (cz + 4) * cy, cx), f32),
            pltpu.VMEM((nv, (cy + 4) * cz, cx), f32),
            pltpu.VMEM((3, pack, rows), f32),
            pltpu.VMEM((nv, rows, cx), f32),
            pltpu.VMEM((nv, rows, cx), f32),
            pltpu.VMEM((nv, rows, cx), f32),
            pltpu.VMEM((nv, rows, cx), f32),
            pltpu.VMEM((rows, cx), f32),
            pltpu.VMEM((nv, nd * cz, rows), bf16),
            pltpu.VMEM((nv, nd * cz, rows), bf16),
            pltpu.VMEM((nv, nz * cy, width), bf16),
            pltpu.VMEM((nv, rows, width), bf16),
            pltpu.VMEM((nv, rows, width), bf16),
            pltpu.VMEM((nv, rows, rows), bf16),
            pltpu.VMEM((nv, rows, rows), bf16),
            pltpu.VMEM((cz, rows), f32),
            pltpu.VMEM((nv, 2, cz, width), f32),
            pltpu.VMEM((cx, gx * pack), f32),
            pltpu.VMEM((cx, nv * cx), f32),
            pltpu.VMEM((gx, pack, rows), f32),
            pltpu.VMEM((nv, gy, nc * cz, cx), f32),
            pltpu.VMEM((nv, gy, nc * cz, cx), f32),
            pltpu.VMEM((nv, gz, 2 * cy, cx), f32),
            pltpu.VMEM((nv, gz, 2 * cy, cx), f32),
            pltpu.VMEM((gz, 2 * cy, cx), f32),
            pltpu.VMEM((gz, 2 * cy, cx), f32),
            pltpu.VMEM((gx, 8, cx), f32),
            pltpu.VMEM((gy, 8, cx), f32),
            pltpu.VMEM((gz, 8, cx), f32),
            pltpu.VMEM(inverse_x.shape, f32),
            pltpu.VMEM(inverse_y.shape, f32),
            pltpu.VMEM(inverse_z.shape, f32),
            pltpu.VMEM(reduced_x.shape, f32),
            pltpu.VMEM(reduced_y.shape, f32),
            pltpu.VMEM(reduced_z.shape, f32),
            pltpu.SMEM(advection.shape, f32),
            dma((nv,)),
            dma((7,)),
            dma((6,)), dma((6,)),
            dma((gx - 1,)), dma((gx - 1,)),
            dma((nv, gy - 1)), dma((nv, gy - 1)),
            dma((nv, gz - 1)), dma((nv, gz - 1)),
            dma((gz - 1,)), dma((gz - 1,)),
            dma((3, most)), dma((3, most)),
        ],
        compiler_params=pltpu.CompilerParams(
            collective_id=0, has_side_effects=True, vmem_limit_bytes=60 * 1024 * 1024),
    )(flow_state.reshape(nv, rows, cx), advection, inverse_x, inverse_y, inverse_z, reduced_x, reduced_y, reduced_z)
    update, norm = pl.pallas_call(
        functools.partial(finish, nv),
        out_shape=(jax.ShapeDtypeStruct((nv, rows, cx), f32), jax.ShapeDtypeStruct((nv,), f32)),
        in_specs=[vmem, vmem],
        out_specs=(pl.BlockSpec(memory_space=pltpu.HBM), pl.BlockSpec(memory_space=pltpu.SMEM)),
        scratch_shapes=[dma((nv,))],
        compiler_params=pltpu.CompilerParams(vmem_limit_bytes=4 * 1024 * 1024),
    )(out, stats)
    return update.reshape(flow_state.shape), norm


def solution(mesh):
    counts = tuple(mesh.shape[axis] for axis in AXES)
    placed = (P(None, "gz", "gy", "gx"), P(), P(), P(), P(), P(), P(), P())
    return jax.shard_map(
        functools.partial(shards, counts),
        mesh=mesh,
        in_specs=placed,
        out_specs=(P(None, "gz", "gy", "gx"), P()),
        check_vma=False,
    )
```

time: 55 us -> 43 us (0.78)
  Pallas kernels: 49.2 us -> 42.2 us
  other arithmetic: 3.1 us -> 0 us
  local copies, waits for them, and re-layouts: 1.82 us -> 0 us
    pallas_call x1, Pallas kernels: 49.2 us -> 40.6 us  [shards(): pl.pallas_call(functools.partial(kernel, (counts, nv, cz, cy, cx, cells))...]
    mul x1 -> x0, other arithmetic: 3.1 us -> none  [shards(): update = (out * stats[5, 0]).reshape(flow_state.shape)]
    slice x2 -> x0, local copies, waits for them, and re-layouts: 1.82 us -> none  [the longest x1 1.19 us: shards(): update = (out * stats[5, 0]).reshape(flow_state.shape)]
    pallas_call x0 -> x1, Pallas kernels: none -> 1.61 us  [shards(): pl.pallas_call(functools.partial(finish, nv), out_shape=(jax.ShapeDtypeSt...]
where the time goes in v1:
time: 43 us; the launch traced here: 42.8 us
  Pallas kernels  42.2 us (98%)
  between operations  0.64 us (1%)
    pallas_call x1, Pallas kernels, shards(): pl.pallas_call(functools.partial(kernel, (counts, nv, cz, cy, cx, cells))...  40.6 us
    pallas_call x1, Pallas kernels, shards(): pl.pallas_call(functools.partial(finish, nv), out_shape=(jax.ShapeDtypeSt...  1.61 us

profile of v1, /device:TPU:0, one launch (start us, length us, event | category | flops | bytes accessed | tf_op | source)
XLA Modules:
  0.0 42.8 jit_solution(1901042051101851938)
XLA Ops:
  0.6 40.6 %shard_map.95 = (f32[5,512,128]{2,1,0:T(8,128)S(1)}, f32[8,128]{1,0:T(8,128)S(1)}) custom-call(f32[5,512,128]{2,1,0:T(8,128)} %bitcast.2, f32[3,5]{1,0:T(4,128)} %adv_h.1, f32[5,128,128]{2,1,0:T(8,128)} %ax_h.1, f32[5,16,16]{2,1,0:T(8,128)} %ay_h.1, f32[5,32,32]{2,1,0:T(8,128)} %az_h.1, f32[5,16,16]{2,1,0:T(8,128)} %rx_h.1, f32[5,8,8]{2,1,0:T(8,128)} %ry_h.1, ...), custom_call_target="tpu_custom_call" | custom-call | tf_op jit(solution)/shard_map/pallas_call | solution.py:513
  41.2 1.6 %shard_map.96 = (f32[5,512,128]{2,1,0:T(8,128)}, f32[5]{0:T(128)}) custom-call(f32[5,512,128]{2,1,0:T(8,128)S(1)} %get-tuple-element.6.solved, f32[8,128]{1,0:T(8,128)S(1)} %get-tuple-element.7.stats), custom_call_target="tpu_custom_call" | custom-call | tf_op jit(solution)/shard_map/pallas_call | solution.py:567

commit v2 on v1

--- a/solution.py
+++ b/solution.py
@@ -92,7 +92,7 @@
 
 
 def kernel(dims, state_h, adv_h, ax_h, ay_h, az_h, rx_h, ry_h, rz_h, out, stats_out,
-           uz, uy, hx, res, edge, field, first, ext, wyh, wyl, wts, pts, pto, khi, klo, azx, kue, mb, cxf,
+           uz, uy, hx, res, edge, field, first, ext, wys, wts, pts, pto, kzh, kzl, kyh, kyl, axs, cyt, mb, cxf,
            xb, ysend, yrecv, zsend, zrecv, esend, erecv, stx, sty, stz,
            ax, ay, az, rx, ry, rz, adv,
            in_sem, aux_sem, halo_send, halo_recv, xs, xr, ys, yr, zs, zr, es, er, ss, sr):
@@ -188,33 +188,59 @@
     for copy in aux:
         copy.wait()
 
-    spread_z = ones_where(iota((cz, rows), 1) // cy == iota((cz, rows), 0))
-    spread_y = ones_where(lax.rem(iota((cy, rows), 1), cy) == iota((cy, rows), 0))
-    for v in range(nv):
-        azx[...] = exact_dot(az[v], spread_z)
-        wide_y = exact_dot(ay[v], spread_y)
-
-        @pl.loop(0, cz)
-        def _(z):
-            high, low = halves(azx[pl.ds(z, 1), :] * wide_y)
-            at = pl.ds(pl.multiple_of(z * cy, cy), cy)
-            khi[v, at, :] = high
-            klo[v, at, :] = low
-
-    nd = wyh.shape[1] // cz
+    every = range(nv)
+    octets = cy // 8
+    group = kyh.shape[1]
+    planes = group // cy
+    groups = cz // planes
+
+    def tall(a, times):
+        return jnp.broadcast_to(a[:, None, :], (a.shape[0], times, a.shape[1])).reshape(a.shape[0] * times, a.shape[1])
+
+    def again(a, times):
+        return jnp.broadcast_to(a[None], (times,) + a.shape).reshape(times * a.shape[0], a.shape[1])
+
+    size_z = kzh.shape[1]
+    spread_z = ones_where(iota((cz, size_z), 1) // 8 == iota((cz, size_z), 0))
+    spread_y = ones_where(lax.rem(iota((cy, group), 1), cy) == iota((cy, group), 0))
+    wide_z = [exact_dot(az[v], spread_z) for v in every]
+    wide_y = [exact_dot(ay[v], spread_y) for v in every]
+    keep_z = lax.rem(iota((size_z, size_z), 0), 8) == lax.rem(iota((size_z, size_z), 1), 8)
+    keep_y = iota((group, group), 0) // cy == iota((group, group), 1) // cy
+    for v in every:
+        kzh[v], kzl[v] = halves(jnp.where(keep_z, tall(wide_z[v], 8), 0.0))
+        kyh[v], kyl[v] = halves(jnp.where(keep_y, again(wide_y[v], planes), 0.0))
+        high, low = halves(ax[v])
+        axs[v, 0:cx] = jnp.concatenate([high, high], axis=1)
+        axs[v, cx:2 * cx] = jnp.concatenate([low, jnp.zeros_like(low)], axis=1)
+
+    nd = wys.shape[1] // cz
     row_y, col_y = iota((nd, 4 * gy), 0), iota((nd, 4 * gy), 1)
     block_y = row_y // nc
     part_y = row_y % nc + (jnp.where(block_y == 0, 2, 0) if nc == 2 else 0)
-    pick_y = iota((4 * gy, 8), 0)
-    pick_y = ones_where((pick_y == 4 * me[1] + iota((4 * gy, 8), 1)) & (iota((4 * gy, 8), 1) < 4))
-    same_z = iota((cz, rows), 1) // cy == iota((cz, rows), 0)
-    for v in range(nv):
-        response = exact_dot(exact_dot(ry[v], pick_y), exact_dot(face_pick((8, cy), cy), ay[v]))
-        wide = exact_dot(exact_dot(coupled(col_y, block_y, part_y, adv[1, v]), response), spread_y)
+    pick_y = ones_where((iota((4 * gy, 8), 0) == 4 * me[1] + iota((4 * gy, 8), 1)) & (iota((4 * gy, 8), 1) < 4))
+    width_y = wys.shape[2]
+    tiled_y = ones_where(lax.rem(iota((8, width_y), 1), 4 * cz) // cz == iota((8, width_y), 0))
+    low_y = iota((1, width_y), 1) >= 8 * cz
+    same_z = iota((cz, width_y), 0) == lax.rem(iota((cz, width_y), 1), cz)
+
+    def stacked(a, low_lane):
+        high = a.astype(bf16).astype(f32)
+        return jnp.where(low_lane, a - high, high)
+
+    near_y = [exact_dot(ry[v], pick_y) for v in every]
+    given = [exact_dot(coupled(col_y, block_y, part_y, adv[1, v]), near_y[v]) for v in every]
+    given = [stacked(exact_dot(given[v], tiled_y), low_y) for v in every]
+    mark_y = iota((cy, nc * cx), 1) // cx
+    if nc == 2:
+        mark_y = jnp.where(me[1] == 0, cy - 2, 0) + mark_y
+    else:
+        mark_y = jnp.where(mark_y < 2, mark_y, cy - 4 + mark_y)
+    mark_y = ones_where(iota((cy, nc * cx), 0) == mark_y)
+    for v in every:
         for n in range(nd):
-            high, low = halves(jnp.where(same_z, wide[n:n + 1, :], 0.0))
-            wyh[v, pl.ds(n * cz, cz), :] = high
-            wyl[v, pl.ds(n * cz, cz), :] = low
+            wys[v, pl.ds(n * cz, cz), :] = jnp.where(same_z, given[v][n:n + 1, :], 0.0).astype(bf16)
+        cyt[v] = exact_dot(ay[v], mark_y)
 
     nz = wts.shape[1] // cy
     row_z, col_z = iota((nz, 4 * gz), 0), iota((nz, 4 * gz), 1)
@@ -227,14 +253,12 @@
     low_lane = iota((1, width), 1) >= 2 * plane4
     same_y = lax.rem(iota((cy, width), 1), cy) == iota((cy, width), 0)
 
-    def stacked(a):
-        high = a.astype(bf16).astype(f32)
-        return jnp.where(low_lane, a - high, high)
-
-    for v in range(nv):
-        given = stacked(exact_dot(exact_dot(sel_z, exact_dot(rz[v], pick_z)), tiled))
+    given = [exact_dot(rz[v], pick_z) for v in every]
+    given = [exact_dot(sel_z, given[v]) for v in every]
+    given = [stacked(exact_dot(given[v], tiled), low_lane) for v in every]
+    for v in every:
         for n in range(nz):
-            wts[v, pl.ds(n * cy, cy), :] = jnp.where(same_y, given[n:n + 1, :], 0.0).astype(bf16)
+            wts[v, pl.ds(n * cy, cy), :] = jnp.where(same_y, given[v][n:n + 1, :], 0.0).astype(bf16)
 
     def part(u, direction):
         ahead = fluxes(u[1], direction)
@@ -280,7 +304,7 @@
         parts = jnp.concatenate([high, mid, both - high - mid, jnp.zeros_like(both)], axis=0).astype(bf16)
         edge[v] = one_dot(parts, weights, TN)
 
-    step = 2 * cy
+    step = cy
     lane = iota((step, cx), 1)
 
     def shifted(a, offset):
@@ -314,19 +338,60 @@
         return tuple(new_squares), top
 
     zero = jnp.zeros((step, cx), f32)
-    last = cz // 2 - 1
-    carry = lax.fori_loop(1, last, body, ((zero,) * nv, zero))
+    carry = lax.fori_loop(2, cz - 2, body, ((zero,) * nv, zero))
     for copy in z_halo:
         copy.wait_recv()
-    squares, top = lax.fori_loop(0, 2, lambda j, c: body(j * last, c), carry)
-
-    y_copies = []
-    for v in range(nv):
-        inner = split_dot(halves(res[v]), halves(ax[v]), NT)
-        first[v] = inner
-        ysend[v] = split_dot((wyh[v], wyl[v]), halves(inner))[0:gy * nc * cz].reshape(gy, nc * cz, cx)
+    squares, top = lax.fori_loop(0, 4, lambda j, c: body(jnp.where(j < 2, j, cz - 4 + j), c), carry)
+
+    y_copies, z_copies = [], []
+
+    def local_x(v):
+        both = one_dot(jnp.concatenate(halves(res[v]), axis=1), axs[v], NT)
+        res[v] = both[:, 0:cx] + both[:, cx:2 * cx]
+
+    def local_y(v):
+        wide = [jnp.concatenate([a[i * group:(i + 1) * group] for i in range(groups)], axis=1) for a in halves(res[v])]
+        solved = split_dot((kyh[v], kyl[v]), wide)
+        for i in range(groups):
+            first[v, pl.ds(i * group, group), :] = solved[:, i * cx:(i + 1) * cx]
+
+    def send_y(v):
+        ends = jnp.concatenate(
+            [first[v, pl.ds(mark, cz, stride=cy), :] for mark in (0, 1, cy - 2, cy - 1)], axis=0)
+        ysend[v] = one_dot(wys[v], stack3(ends))[0:gy * nc * cz].reshape(gy, nc * cz, cx)
         y_copies.append(spread(1, lambda t: ysend.at[v, t], yrecv.at[v, me[1]],
                                lambda k: ys.at[v, k], lambda k: yr.at[v, k]))
+
+    def solve_z(v):
+        for copy in y_copies[v]:
+            copy.wait_recv()
+        taken = ysend[v, me[1]]
+        for k in range(1, gy):
+            taken = taken + yrecv[v, lax.rem(me[1] + k, gy)]
+        value = first[v].reshape(cz, cy, cx)
+        for c in range(nc):
+            value = value - cyt[v, :, c * cx:(c + 1) * cx][None] * taken[c * cz:(c + 1) * cz][:, None, :]
+        wide = jnp.concatenate(
+            [value[:, 8 * i:8 * i + 8, :].reshape(size_z, cx) for i in range(octets)], axis=1)
+        solved = split_dot((kzh[v], kzl[v]), halves(wide))
+        for i in range(octets):
+            field[v, :, 8 * i:8 * i + 8, :] = solved[:, i * cx:(i + 1) * cx].reshape(cz, 8, cx)
+
+    def end_planes(v):
+        return jnp.concatenate([field[v, 0:2].reshape(2 * cy, cx), field[v, cz - 2:cz].reshape(2 * cy, cx)], axis=0)
+
+    def send_z(v):
+        zsend[v] = one_dot(wts[v], stack3(end_planes(v)))[0:gz * 2 * cy].reshape(gz, 2 * cy, cx)
+        z_copies.append(spread(2, lambda t: zsend.at[v, t], zrecv.at[v, me[2]],
+                               lambda k: zs.at[v, k], lambda k: zr.at[v, k]))
+
+    def in_turn(stages):
+        for turn in range(nv + len(stages) - 1):
+            for back, stage in enumerate(stages):
+                if 0 <= turn - back < nv:
+                    stage(turn - back)
+
+    in_turn([local_x, local_y, send_y])
 
     sub_s = iota((8, cx), 0)
     tile = jnp.where(sub_s == 5, jnp.max(top, axis=0, keepdims=True), 0.0)
@@ -341,26 +406,9 @@
             result = jnp.where(sub_s < nv, result + ref[q], jnp.maximum(result, ref[q]))
         return result
 
-    def end_planes(ref, v):
-        return jnp.concatenate([ref[v, pl.ds(0, 2 * cy), :], ref[v, pl.ds((cz - 2) * cy, 2 * cy), :]], axis=0)
-
-    z_copies = []
-    for v in range(nv):
-        for copy in y_copies[v]:
-            copy.wait_recv()
-        taken = ysend[v, me[1]]
-        for k in range(1, gy):
-            taken = taken + yrecv[v, lax.rem(me[1] + k, gy)]
-        start = jnp.where(me[1] == 0, cy - 2, 0)
-        for c in range(nc):
-            at = pl.ds(start + c, cz, stride=cy) if nc == 2 else pl.ds(c if c < 2 else cy - 4 + c, cz, stride=cy)
-            first[v, at, :] = first[v, at, :] - taken[c * cz:(c + 1) * cz]
-        field[v] = split_dot((khi[v], klo[v]), halves(first[v]))
-        zsend[v] = one_dot(wts[v], stack3(end_planes(field, v)))[0:gz * 2 * cy].reshape(gz, 2 * cy, cx)
-        z_copies.append(spread(2, lambda t: zsend.at[v, t], zrecv.at[v, me[2]],
-                               lambda k: zs.at[v, k], lambda k: zr.at[v, k]))
-
-    xb[me[0]] = faces_to_rows(lambda v: field[v])
+    in_turn([solve_z, send_z])
+
+    xb[me[0]] = faces_to_rows(lambda v: field[v].reshape(rows, cx))
     x_copies = [spread(0, lambda t: xb.at[me[0]], xb.at[me[0]], lambda k: xs.at[k], lambda k: xr.at[k])]
     for copy in stat_copies[0]:
         copy.wait_recv()
@@ -373,26 +421,29 @@
     in_x = lax.rem(iota((4 * gx, wide_x), 1), pack)
     block_x = iota((4 * gx, wide_x), 1) // pack
     row_x = iota((8, 4 * gx), 0)
-    for v in range(nv):
-        m = exact_dot(coupled(iota((8, 4 * gx), 1), me[0], row_x, adv[0, v]), rx[v])
-        to_pack = ones_where((in_x // 4 == v) & (iota((4 * gx, wide_x), 0) == 4 * block_x + lax.rem(in_x + 2, 4)))
-        placed = exact_dot(m, to_pack)
-        columns = exact_dot(face_pick((8, cx), cx), ax[v], NT)
-        high = columns.astype(bf16).astype(f32)
+    placed = [exact_dot(coupled(iota((8, 4 * gx), 1), me[0], row_x, adv[0, v]), rx[v]) for v in every]
+    to_pack = [ones_where((in_x // 4 == v) & (iota((4 * gx, wide_x), 0) == 4 * block_x + lax.rem(in_x + 2, 4)))
+               for v in every]
+    placed = [exact_dot(placed[v], to_pack[v]) for v in every]
+    columns = [exact_dot(face_pick((8, cx), cx), ax[v], NT) for v in every]
+    for v in every:
+        high = columns[v].astype(bf16).astype(f32)
         for k in range(3):
             at = pl.ds(4 * v + 32 * k, 4)
-            mb[at, :] = placed[0:4]
-            cxf[at, v * cx:(v + 1) * cx] = (high if k < 2 else columns - high)[0:4]
+            mb[at, :] = placed[v][0:4]
+            cxf[at, v * cx:(v + 1) * cx] = (high if k < 2 else columns[v] - high)[0:4]
 
     row_l, col_l = iota((8, 4 * gz), 0), iota((8, 4 * gz), 1)
     sel_lf = ones_where((row_l < 4) & (col_l == 4 * me[2] + jnp.where(row_l < 2, row_l - 2, row_l + 2)))
     r8, c8 = iota((8, 8), 0), iota((8, 8), 1)
-    for v in range(nv):
-        near = exact_dot(sel_lf, rz[v])
-        square = exact_dot(near, sel_lf, NT)
-
+    near = [exact_dot(sel_lf, rz[v]) for v in every]
+    square = [exact_dot(near[v], sel_lf, NT) for v in every]
+    own = [exact_dot(near[v], pick_z) for v in every]
+    columns = [exact_dot(az[v], face_pick((8, cz), cz), NT) for v in every]
+
+    def mixed(v):
         def e(i, j):
-            return square[i:i + 1, j:j + 1]
+            return square[v][i:i + 1, j:j + 1]
 
         det_l = e(0, 0) * e(1, 1) - e(0, 1) * e(1, 0)
         det_f = e(2, 2) * e(3, 3) - e(2, 3) * e(3, 2)
@@ -406,25 +457,27 @@
             for j, value in enumerate([(e(i, 2) * e(3, 3) - e(i, 3) * e(3, 2)) * inv_f,
                                        (e(i, 3) * e(2, 2) - e(i, 2) * e(2, 3)) * inv_f]):
                 mix = jnp.where((r8 == i) & (c8 == 2 + j), value, mix)
+        return mix
+
+    def weighed(v):
         speed = adv[2, v]
         weigh = jnp.where((r8 == c8) & (r8 < 4), fourth_coef, 0.0)
         weigh = jnp.where((r8 == 0) & (c8 == 1), -0.5 * speed - 4.0 * fourth_coef, weigh)
-        weigh = jnp.where((r8 == 3) & (c8 == 2), 0.5 * speed - 4.0 * fourth_coef, weigh).astype(f32)
-        columns = exact_dot(az[v], face_pick((8, cz), cz), NT)
-        peers = exact_dot(weigh, mix)
-        own = exact_dot(weigh, exact_dot(near, pick_z))
-        kue[v, 0] = stacked(exact_dot(exact_dot(columns, peers), tiled))
-        kue[v, 1] = stacked(exact_dot(exact_dot(columns, own), tiled))
-
-    @pl.loop(0, cz)
-    def _(z):
-        at = pl.ds(pl.multiple_of(z * cy, cy), cy)
-        for v in range(nv):
-            pts[v, at, :] = jnp.where(same_y, kue[v, 0, pl.ds(z, 1), :], 0.0).astype(bf16)
-            pto[v, at, :] = jnp.where(same_y, kue[v, 1, pl.ds(z, 1), :], 0.0).astype(bf16)
-
-    for v in range(nv):
-        field[v] = field[v] - one_dot(pto[v], stack3(end_planes(field, v)))
+        return jnp.where((r8 == 3) & (c8 == 2), 0.5 * speed - 4.0 * fourth_coef, weigh).astype(f32)
+
+    own = [exact_dot(weighed(v), own[v]) for v in every]
+    peers = [exact_dot(weighed(v), mixed(v)) for v in every]
+    own = [exact_dot(own[v], tiled) for v in every]
+    peers = [exact_dot(peers[v], tiled) for v in every]
+    own = [stacked(exact_dot(columns[v], own[v]), low_lane) for v in every]
+    peers = [stacked(exact_dot(columns[v], peers[v]), low_lane) for v in every]
+    for v in every:
+        for z in range(cz):
+            pto[v, pl.ds(z * cy, cy), :] = jnp.where(same_y, own[v][z:z + 1, :], 0.0).astype(bf16)
+            pts[v, pl.ds(z * cy, cy), :] = jnp.where(same_y, peers[v][z:z + 1, :], 0.0).astype(bf16)
+
+    for v in every:
+        field[v] = field[v] - one_dot(pto[v], stack3(end_planes(v))).reshape(cz, cy, cx)
 
     for group in x_copies + [stat_copies[1]]:
         for copy in group:
@@ -461,7 +514,7 @@
     for v in range(nv):
         for copy in z_copies[v]:
             copy.wait_recv()
-        field[v] = field[v] - one_dot(pts[v], stack3(sides(lambda q: zrecv[v, q])))
+        field[v] = field[v] - one_dot(pts[v], stack3(sides(lambda q: zrecv[v, q]))).reshape(cz, cy, cx)
 
     for copy in stat_copies[2]:
         copy.wait_recv()
@@ -477,7 +530,7 @@
     high = solved.astype(bf16).astype(f32)
     parts = jnp.where((lane_c >= 32) & (lane_c < 64), solved - high, high).astype(bf16)
     for v in range(nv):
-        out[v] = (field[v] - one_dot(parts, cxf[:, v * cx:(v + 1) * cx].astype(bf16))) * time_step
+        out[v] = (field[v].reshape(rows, cx) - one_dot(parts, cxf[:, v * cx:(v + 1) * cx].astype(bf16))) * time_step
 
     for group in [x_halo, y_halo, z_halo, e_copies] + x_copies + y_copies + z_copies + stat_copies:
         for copy in group:
@@ -510,6 +563,7 @@
     nd = max(8, gy * nc)
     nz = max(8, 2 * gz)
     width = 12 * cy
+    group = cy * min(cz, max(1, 256 // cy))
     out, stats = pl.pallas_call(
         functools.partial(kernel, (counts, nv, cz, cy, cx, cells)),
         out_shape=(pltpu.VMEM((nv, rows, cx), f32), pltpu.VMEM((8, cx), f32)),
@@ -521,18 +575,19 @@
             pltpu.VMEM((3, pack, rows), f32),
             pltpu.VMEM((nv, rows, cx), f32),
             pltpu.VMEM((nv, rows, cx), f32),
-            pltpu.VMEM((nv, rows, cx), f32),
+            pltpu.VMEM((nv, cz, cy, cx), f32),
             pltpu.VMEM((nv, rows, cx), f32),
             pltpu.VMEM((rows, cx), f32),
-            pltpu.VMEM((nv, nd * cz, rows), bf16),
-            pltpu.VMEM((nv, nd * cz, rows), bf16),
+            pltpu.VMEM((nv, nd * cz, 12 * cz), bf16),
             pltpu.VMEM((nv, nz * cy, width), bf16),
             pltpu.VMEM((nv, rows, width), bf16),
             pltpu.VMEM((nv, rows, width), bf16),
-            pltpu.VMEM((nv, rows, rows), bf16),
-            pltpu.VMEM((nv, rows, rows), bf16),
-            pltpu.VMEM((cz, rows), f32),
-            pltpu.VMEM((nv, 2, cz, width), f32),
+            pltpu.VMEM((nv, 8 * cz, 8 * cz), bf16),
+            pltpu.VMEM((nv, 8 * cz, 8 * cz), bf16),
+            pltpu.VMEM((nv, group, group), bf16),
+            pltpu.VMEM((nv, group, group), bf16),
+            pltpu.VMEM((nv, 2 * cx, 2 * cx), bf16),
+            pltpu.VMEM((nv, cy, nc * cx), f32),
             pltpu.VMEM((cx, gx * pack), f32),
             pltpu.VMEM((cx, nv * cx), f32),
             pltpu.VMEM((gx, pack, rows), f32),

time: 43 us -> 32.8 us (0.76)
  Pallas kernels: 42.2 us -> 32 us
    pallas_call x1, Pallas kernels: 40.6 us -> 30.4 us  [shards(): pl.pallas_call(functools.partial(kernel, (counts, nv, cz, cy, cx, cells))...]
where the time goes in v2:
time: 32.8 us; the launch traced here: 32.6 us
  Pallas kernels  32 us (98%)
  between operations  0.64 us (2%)
    pallas_call x1, Pallas kernels, shards(): pl.pallas_call(functools.partial(kernel, (counts, nv, cz, cy, cx, cells))...  30.4 us
    pallas_call x1, Pallas kernels, shards(): pl.pallas_call(functools.partial(finish, nv), out_shape=(jax.ShapeDtypeSt...  1.61 us

profile of v2, /device:TPU:0, one launch (start us, length us, event | category | flops | bytes accessed | tf_op | source)
XLA Modules:
  0.0 32.6 jit_solution(15101828761025969228)
XLA Ops:
  0.6 30.4 %shard_map.95 = (f32[5,512,128]{2,1,0:T(8,128)S(1)}, f32[8,128]{1,0:T(8,128)S(1)}) custom-call(f32[5,512,128]{2,1,0:T(8,128)} %bitcast.2, f32[3,5]{1,0:T(4,128)} %adv_h.1, f32[5,128,128]{2,1,0:T(8,128)} %ax_h.1, f32[5,16,16]{2,1,0:T(8,128)} %ay_h.1, f32[5,32,32]{2,1,0:T(8,128)} %az_h.1, f32[5,16,16]{2,1,0:T(8,128)} %rx_h.1, f32[5,8,8]{2,1,0:T(8,128)} %ry_h.1, ...), custom_call_target="tpu_custom_call" | custom-call | tf_op jit(solution)/shard_map/pallas_call | solution.py:567
  31.0 1.6 %shard_map.96 = (f32[5,512,128]{2,1,0:T(8,128)}, f32[5]{0:T(128)}) custom-call(f32[5,512,128]{2,1,0:T(8,128)S(1)} %get-tuple-element.6.solved, f32[8,128]{1,0:T(8,128)S(1)} %get-tuple-element.7.stats), custom_call_target="tpu_custom_call" | custom-call | tf_op jit(solution)/shard_map/pallas_call | solution.py:622

commit v3 on v2

--- a/solution.py
+++ b/solution.py
@@ -92,7 +92,7 @@
 
 
 def kernel(dims, state_h, adv_h, ax_h, ay_h, az_h, rx_h, ry_h, rz_h, out, stats_out,
-           uz, uy, hx, res, edge, field, first, ext, wys, wts, pts, pto, kzh, kzl, kyh, kyl, axs, cyt, mb, cxf,
+           uz, uy, vel, prs, hx, res, edge, field, first, ext, wys, wts, pts, pto, kzh, kzl, kyh, kyl, axs, cyt, mb, cxf, cxb,
            xb, ysend, yrecv, zsend, zrecv, esend, erecv, stx, sty, stz,
            ax, ay, az, rx, ry, rz, adv,
            in_sem, aux_sem, halo_send, halo_recv, xs, xr, ys, yr, zs, zr, es, er, ss, sr):
@@ -133,7 +133,6 @@
             packed = jnp.where(lane_c // 4 == v, moved, packed)
         return jnp.transpose(packed)[0:pack]
 
-    hx[0] = faces_to_rows(lambda v: uz[v, pl.ds(2 * cy, rows), :])
     pl.semaphore_wait(barrier, total)
 
     def ring(axis, slot, down_src, down_dst, up_src, up_dst, far_first=False):
@@ -176,6 +175,8 @@
     z_halo = ring(2, 4,
                   uz.at[:, pl.ds(2 * cy, 2 * cy)], uz.at[:, pl.ds((cz + 2) * cy, 2 * cy)],
                   uz.at[:, pl.ds(cz * cy, 2 * cy)], uz.at[:, pl.ds(0, 2 * cy)], far_first=True)
+    hx[0] = faces_to_rows(lambda v: uz[v, pl.ds(2 * cy, rows), :])
+
     x_halo = ring(0, 0, hx.at[0], hx.at[1], hx.at[0], hx.at[2])
 
     for v in range(nv):
@@ -184,6 +185,21 @@
     y_halo = ring(1, 2,
                   uy.at[:, pl.ds(2 * cz, 2 * cz)], uy.at[:, pl.ds((cy + 2) * cz, 2 * cz)],
                   uy.at[:, pl.ds(cy * cz, 2 * cz)], uy.at[:, pl.ds(0, 2 * cz)])
+
+    def derive(start, size):
+        at = pl.ds(start, size)
+        velocity, internal, pressure = primitives([uz[v, at, :] for v in range(nv)])
+        for j in range(3):
+            vel[j, at, :] = velocity[j]
+        prs[at, :] = pressure
+        return (jnp.abs(velocity[0]) + jnp.abs(velocity[1]) + jnp.abs(velocity[2])
+                + jnp.sqrt(3.0 * 1.4 * gas_ratio * internal))
+
+    chunk = 4 * cy
+    top = lax.fori_loop(
+        0, rows // chunk,
+        lambda i, top: jnp.maximum(top, derive(pl.multiple_of(2 * cy + i * chunk, 8), chunk)),
+        jnp.zeros((chunk, cx), f32))
 
     for copy in aux:
         copy.wait()
@@ -286,7 +302,9 @@
         copy.wait_recv()
     sub4 = iota((4, rows), 0)
     merged = [jnp.where(sub4 < 2, hx[2, 4 * v:4 * v + 4, :], hx[1, 4 * v:4 * v + 4, :]) for v in range(nv)]
-    halo_flux = fluxes(merged, 0)
+    nearest = [hx[0, 4 * v:4 * v + 4, :] for v in range(nv)]
+    halo_flux = [a - b for a, b in zip(fluxes(merged, 0), fluxes(nearest, 0))]
+    merged = [a - b for a, b in zip(merged, nearest)]
     sub8, lane8 = iota((8, cx), 0), iota((8, cx), 1)
 
     def at_lane(row, lane, value):
@@ -304,44 +322,54 @@
         parts = jnp.concatenate([high, mid, both - high - mid, jnp.zeros_like(both)], axis=0).astype(bf16)
         edge[v] = one_dot(parts, weights, TN)
 
-    step = cy
-    lane = iota((step, cx), 1)
-
-    def shifted(a, offset):
-        moved = pltpu.roll(a, (-offset) % cx, 1)
-        inside = lane < cx - offset if offset > 0 else lane >= -offset
-        return jnp.where(inside, moved, 0.0)
-
-    def body(i, carry):
-        squares, top = carry
-        base = pl.multiple_of(i * step, step)
-        u = {}
-        for off in range(-2, 3):
-            at = pl.ds(pl.multiple_of(base + (off + 2) * cy, cy), step)
-            u[off] = [uz[v, at, :] for v in range(nv)]
-        found = part(u, 2)
-        values = primitives(u[0])
-        velocity, internal, _ = values
-        wave = (jnp.abs(velocity[0]) + jnp.abs(velocity[1]) + jnp.abs(velocity[2])
-                + jnp.sqrt(3.0 * 1.4 * gas_ratio * internal))
-        top = jnp.maximum(top, wave)
-        flux_x = fluxes(u[0], 0, values)
-        new_squares = []
+    def residual(base, planes, squares):
+        size = planes * cy
+        here = pl.ds(base + 2 * cy, size)
+        vx, pc = vel[0, here, :], prs[here, :]
+        around = pl.ds(base + cy, size + 2 * cy)
+        vz, pz = vel[2, around, :], prs[around, :]
+        found = []
         for v in range(nv):
-            c = u[0][v]
-            fourth = (shifted(c, -2) + shifted(c, 2)) - 4.0 * (shifted(c, -1) + shifted(c, 1)) + 6.0 * c
-            along_x = -0.5 * (shifted(flux_x[v], 1) - shifted(flux_x[v], -1)) - damping * fourth
-            at = pl.ds(base, step)
-            value = res[v, at, :] + found[v] + (along_x + edge[v, at, :])
+            u = uz[v, pl.ds(base, size + 4 * cy), :]
+            inner = u[cy:size + 3 * cy]
+            c = u[2 * cy:size + 2 * cy]
+            if v == 0:
+                flux_x, flux_z = uz[1, here, :], uz[3, around, :]
+            elif v == 4:
+                flux_x, flux_z = (c + pc) * vx, (inner + pz) * vz
+            else:
+                flux_x = c * vx + pc if v == 1 else c * vx
+                flux_z = inner * vz + pz if v == 3 else inner * vz
+            beside = inner[0:size] + inner[2 * cy:size + 2 * cy]
+            beyond = u[0:size] + u[4 * cy:size + 4 * cy]
+            along_z = 0.5 * (flux_z[0:size] - flux_z[2 * cy:size + 2 * cy]) + (4.0 * damping * beside - damping * beyond)
+            near, half, far = 4.0 * damping * c, 0.5 * flux_x, -damping * c
+            along_x = ((pltpu.roll(near - half, cx - 1, 1) + pltpu.roll(near + half, 1, 1))
+                       + (pltpu.roll(far, cx - 2, 1) + pltpu.roll(far, 2, 1)))
+            at = pl.ds(base, size)
+            value = (res[v, at, :] + edge[v, at, :]) + (along_z + along_x) - 12.0 * damping * c
             res[v, at, :] = value
-            new_squares.append(squares[v] + value * value)
-        return tuple(new_squares), top
-
-    zero = jnp.zeros((step, cx), f32)
-    carry = lax.fori_loop(2, cz - 2, body, ((zero,) * nv, zero))
+            found.append(squares[v] + jnp.sum((value * value).reshape(planes, cy, cx), axis=0))
+        return tuple(found)
+
+    planes_in = next(n for n in (7, 4, 2, 1) if (cz - 4) % n == 0)
+    squares = lax.fori_loop(
+        0, (cz - 4) // planes_in,
+        lambda i, c: residual(pl.multiple_of(2 * cy + i * planes_in * cy, 8), planes_in, c),
+        (jnp.zeros((cy, cx), f32),) * nv)
     for copy in z_halo:
         copy.wait_recv()
-    squares, top = lax.fori_loop(0, 4, lambda j, c: body(jnp.where(j < 2, j, cz - 4 + j), c), carry)
+    derive(0, 2 * cy)
+    derive((cz + 2) * cy, 2 * cy)
+    squares = residual(0, 2, squares)
+    squares = residual((cz - 2) * cy, 2, squares)
+
+    sub_s = iota((8, cx), 0)
+    tile = jnp.where(sub_s == 5, jnp.max(top, axis=0, keepdims=True), 0.0)
+    for v in range(nv):
+        tile = jnp.where(sub_s == v, jnp.sum(squares[v], axis=0, keepdims=True), tile)
+    sty[me[1]] = tile
+    stat_copies = [spread(1, lambda t: sty.at[me[1]], sty.at[me[1]], lambda k: ss.at[0, k], lambda k: sr.at[0, k])]
 
     y_copies, z_copies = [], []
 
@@ -385,28 +413,23 @@
         z_copies.append(spread(2, lambda t: zsend.at[v, t], zrecv.at[v, me[2]],
                                lambda k: zs.at[v, k], lambda k: zr.at[v, k]))
 
-    def in_turn(stages):
-        for turn in range(nv + len(stages) - 1):
-            for back, stage in enumerate(stages):
-                if 0 <= turn - back < nv:
-                    stage(turn - back)
-
-    in_turn([local_x, local_y, send_y])
-
-    sub_s = iota((8, cx), 0)
-    tile = jnp.where(sub_s == 5, jnp.max(top, axis=0, keepdims=True), 0.0)
-    for v in range(nv):
-        tile = jnp.where(sub_s == v, jnp.sum(squares[v], axis=0, keepdims=True), tile)
-    sty[me[1]] = tile
-    stat_copies = [spread(1, lambda t: sty.at[me[1]], sty.at[me[1]], lambda k: ss.at[0, k], lambda k: sr.at[0, k])]
-
     def gathered(ref, count):
         result = ref[0]
         for q in range(1, count):
             result = jnp.where(sub_s < nv, result + ref[q], jnp.maximum(result, ref[q]))
         return result
 
-    in_turn([solve_z, send_z])
+    for turn in range(nv + 2):
+        if turn < nv:
+            local_x(turn)
+        if turn >= 2:
+            solve_z(turn - 2)
+        if turn < nv:
+            local_y(turn)
+        if turn >= 2:
+            send_z(turn - 2)
+        if turn < nv:
+            send_y(turn)
 
     xb[me[0]] = faces_to_rows(lambda v: field[v].reshape(rows, cx))
     x_copies = [spread(0, lambda t: xb.at[me[0]], xb.at[me[0]], lambda k: xs.at[k], lambda k: xr.at[k])]
@@ -432,6 +455,8 @@
             at = pl.ds(4 * v + 32 * k, 4)
             mb[at, :] = placed[v][0:4]
             cxf[at, v * cx:(v + 1) * cx] = (high if k < 2 else columns[v] - high)[0:4]
+
+    cxb[...] = cxf[...].astype(bf16)
 
     row_l, col_l = iota((8, 4 * gz), 0), iota((8, 4 * gz), 1)
     sel_lf = ones_where((row_l < 4) & (col_l == 4 * me[2] + jnp.where(row_l < 2, row_l - 2, row_l + 2)))
@@ -511,10 +536,13 @@
             after = right if after is None else after + right
         return jnp.concatenate([before, after], axis=0)
 
-    for v in range(nv):
-        for copy in z_copies[v]:
-            copy.wait_recv()
-        field[v] = field[v] - one_dot(pts[v], stack3(sides(lambda q: zrecv[v, q]))).reshape(cz, cy, cx)
+    def doubled(a, lanes):
+        high = a.astype(bf16).astype(f32)
+        return jnp.where((lanes >= 32) & (lanes < 64), a - high, high).astype(bf16)
+
+    parts = doubled(ext[...], lane_c)
+    for v in every:
+        field[v] = field[v] - one_dot(parts, cxb[:, v * cx:(v + 1) * cx]).reshape(cz, cy, cx)
 
     for copy in stat_copies[2]:
         copy.wait_recv()
@@ -526,11 +554,13 @@
 
     for copy in e_copies:
         copy.wait_recv()
-    solved = ext[...] - by_variable(pts, sides(lambda q: erecv[q]))
-    high = solved.astype(bf16).astype(f32)
-    parts = jnp.where((lane_c >= 32) & (lane_c < 64), solved - high, high).astype(bf16)
-    for v in range(nv):
-        out[v] = (field[v].reshape(rows, cx) - one_dot(parts, cxf[:, v * cx:(v + 1) * cx].astype(bf16))) * time_step
+    for v in every:
+        for copy in z_copies[v]:
+            copy.wait_recv()
+    parts = doubled(sides(lambda q: erecv[q]), lane_e)
+    shares = [sides(lambda q: zrecv[v, q]) - one_dot(parts, cxb[:, v * cx:(v + 1) * cx]) for v in every]
+    for v in every:
+        out[v] = (field[v].reshape(rows, cx) - one_dot(pts[v], stack3(shares[v]))) * time_step
 
     for group in [x_halo, y_halo, z_halo, e_copies] + x_copies + y_copies + z_copies + stat_copies:
         for copy in group:
@@ -572,6 +602,8 @@
         scratch_shapes=[
             pltpu.VMEM((nv, (cz + 4) * cy, cx), f32),
             pltpu.VMEM((nv, (cy + 4) * cz, cx), f32),
+            pltpu.VMEM((3, (cz + 4) * cy, cx), f32),
+            pltpu.VMEM(((cz + 4) * cy, cx), f32),
             pltpu.VMEM((3, pack, rows), f32),
             pltpu.VMEM((nv, rows, cx), f32),
             pltpu.VMEM((nv, rows, cx), f32),
@@ -590,6 +622,7 @@
             pltpu.VMEM((nv, cy, nc * cx), f32),
             pltpu.VMEM((cx, gx * pack), f32),
             pltpu.VMEM((cx, nv * cx), f32),
+            pltpu.VMEM((cx, nv * cx), bf16),
             pltpu.VMEM((gx, pack, rows), f32),
             pltpu.VMEM((nv, gy, nc * cz, cx), f32),
             pltpu.VMEM((nv, gy, nc * cz, cx), f32),

time: 32.8 us -> 31.6 us (0.963)
  Pallas kernels: 32 us -> 30.8 us
    pallas_call x1, Pallas kernels: 30.4 us -> 29.2 us  [shards(): pl.pallas_call(functools.partial(kernel, (counts, nv, cz, cy, cx, cells))...]
where the time goes in v3:
time: 31.6 us; the launch traced here: 31.5 us
  Pallas kernels  30.8 us (97%)
  between operations  0.64 us (2%)
    pallas_call x1, Pallas kernels, shards(): pl.pallas_call(functools.partial(kernel, (counts, nv, cz, cy, cx, cells))...  29.2 us
    pallas_call x1, Pallas kernels, shards(): pl.pallas_call(functools.partial(finish, nv), out_shape=(jax.ShapeDtypeSt...  1.61 us

profile of v3, /device:TPU:0, one launch (start us, length us, event | category | flops | bytes accessed | tf_op | source)
XLA Modules:
  0.0 31.5 jit_solution(478291613118676257)
XLA Ops:
  0.6 29.2 %shard_map.95 = (f32[5,512,128]{2,1,0:T(8,128)S(1)}, f32[8,128]{1,0:T(8,128)S(1)}) custom-call(f32[5,512,128]{2,1,0:T(8,128)} %bitcast.2, f32[3,5]{1,0:T(4,128)} %adv_h.1, f32[5,128,128]{2,1,0:T(8,128)} %ax_h.1, f32[5,16,16]{2,1,0:T(8,128)} %ay_h.1, f32[5,32,32]{2,1,0:T(8,128)} %az_h.1, f32[5,16,16]{2,1,0:T(8,128)} %rx_h.1, f32[5,8,8]{2,1,0:T(8,128)} %ry_h.1, ...), custom_call_target="tpu_custom_call" | custom-call | tf_op jit(solution)/shard_map/pallas_call | solution.py:597
  29.9 1.6 %shard_map.96 = (f32[5,512,128]{2,1,0:T(8,128)}, f32[5]{0:T(128)}) custom-call(f32[5,512,128]{2,1,0:T(8,128)S(1)} %get-tuple-element.6.solved, f32[8,128]{1,0:T(8,128)S(1)} %get-tuple-element.7.stats), custom_call_target="tpu_custom_call" | custom-call | tf_op jit(solution)/shard_map/pallas_call | solution.py:655

commit v4 on v3

--- a/solution.py
+++ b/solution.py
@@ -92,10 +92,10 @@
 
 
 def kernel(dims, state_h, adv_h, ax_h, ay_h, az_h, rx_h, ry_h, rz_h, out, stats_out,
-           uz, uy, vel, prs, hx, res, edge, field, first, ext, wys, wts, pts, pto, kzh, kzl, kyh, kyl, axs, cyt, mb, cxf, cxb,
-           xb, ysend, yrecv, zsend, zrecv, esend, erecv, stx, sty, stz,
+           uz, uy, vel, prs, hx, res, edge, field, first, ext, wys, wts, pts, pto, kzh, kzl, kyh, kyl, axs, cyt, mb, mw, cxf, cxb,
+           xb, ysend, yrecv, zsend, zrecv, esend, erecv, stp, sty,
            ax, ay, az, rx, ry, rz, adv,
-           in_sem, aux_sem, halo_send, halo_recv, xs, xr, ys, yr, zs, zr, es, er, ss, sr):
+           in_sem, aux_sem, halo_send, halo_recv, xs, xr, ys, yr, zs, zr, es, er, ps, pr, ss, sr, joined):
     counts, nv, cz, cy, cx, cells = dims
     gx, gy, gz = counts
     rows = cz * cy
@@ -126,14 +126,16 @@
 
     lane_c = iota((rows, cx), 1)
 
-    def faces_to_rows(load):
+    def faces_packed(load):
         packed = jnp.zeros((rows, cx), f32)
         for v in range(nv):
             moved = pltpu.roll(load(v), 4 * v + 2, 1)
             packed = jnp.where(lane_c // 4 == v, moved, packed)
-        return jnp.transpose(packed)[0:pack]
+        return packed
 
     pl.semaphore_wait(barrier, total)
+    for k in range(1, gz):
+        pl.semaphore_signal(joined, inc=1, device_id={"gz": lax.rem(me[2] + k, gz)}, device_id_type=MESH)
 
     def ring(axis, slot, down_src, down_dst, up_src, up_dst, far_first=False):
         count, place = counts[axis], me[axis]
@@ -172,10 +174,25 @@
             copies.append(copy)
         return copies
 
+    def across(src, dst, send, recv, same_z):
+        copies = []
+        for kz in range(gz):
+            for kx in range(gx):
+                if kz == 0 and (kx == 0 or not same_z):
+                    continue
+                tx, tz = lax.rem(me[0] + kx, gx), lax.rem(me[2] + kz, gz)
+                n = kz * gx + kx
+                copy = pltpu.make_async_remote_copy(
+                    src_ref=src(tz), dst_ref=dst, send_sem=send.at[n], recv_sem=recv.at[n],
+                    device_id={"gx": tx, "gz": tz}, device_id_type=MESH)
+                copy.start()
+                copies.append(copy)
+        return copies
+
     z_halo = ring(2, 4,
                   uz.at[:, pl.ds(2 * cy, 2 * cy)], uz.at[:, pl.ds((cz + 2) * cy, 2 * cy)],
                   uz.at[:, pl.ds(cz * cy, 2 * cy)], uz.at[:, pl.ds(0, 2 * cy)], far_first=True)
-    hx[0] = faces_to_rows(lambda v: uz[v, pl.ds(2 * cy, rows), :])
+    hx[0] = jnp.transpose(faces_packed(lambda v: uz[v, pl.ds(2 * cy, rows), :]))[0:pack]
 
     x_halo = ring(0, 0, hx.at[0], hx.at[1], hx.at[0], hx.at[2])
 
@@ -219,16 +236,8 @@
     size_z = kzh.shape[1]
     spread_z = ones_where(iota((cz, size_z), 1) // 8 == iota((cz, size_z), 0))
     spread_y = ones_where(lax.rem(iota((cy, group), 1), cy) == iota((cy, group), 0))
-    wide_z = [exact_dot(az[v], spread_z) for v in every]
-    wide_y = [exact_dot(ay[v], spread_y) for v in every]
     keep_z = lax.rem(iota((size_z, size_z), 0), 8) == lax.rem(iota((size_z, size_z), 1), 8)
     keep_y = iota((group, group), 0) // cy == iota((group, group), 1) // cy
-    for v in every:
-        kzh[v], kzl[v] = halves(jnp.where(keep_z, tall(wide_z[v], 8), 0.0))
-        kyh[v], kyl[v] = halves(jnp.where(keep_y, again(wide_y[v], planes), 0.0))
-        high, low = halves(ax[v])
-        axs[v, 0:cx] = jnp.concatenate([high, high], axis=1)
-        axs[v, cx:2 * cx] = jnp.concatenate([low, jnp.zeros_like(low)], axis=1)
 
     nd = wys.shape[1] // cz
     row_y, col_y = iota((nd, 4 * gy), 0), iota((nd, 4 * gy), 1)
@@ -239,24 +248,12 @@
     tiled_y = ones_where(lax.rem(iota((8, width_y), 1), 4 * cz) // cz == iota((8, width_y), 0))
     low_y = iota((1, width_y), 1) >= 8 * cz
     same_z = iota((cz, width_y), 0) == lax.rem(iota((cz, width_y), 1), cz)
-
-    def stacked(a, low_lane):
-        high = a.astype(bf16).astype(f32)
-        return jnp.where(low_lane, a - high, high)
-
-    near_y = [exact_dot(ry[v], pick_y) for v in every]
-    given = [exact_dot(coupled(col_y, block_y, part_y, adv[1, v]), near_y[v]) for v in every]
-    given = [stacked(exact_dot(given[v], tiled_y), low_y) for v in every]
     mark_y = iota((cy, nc * cx), 1) // cx
     if nc == 2:
         mark_y = jnp.where(me[1] == 0, cy - 2, 0) + mark_y
     else:
         mark_y = jnp.where(mark_y < 2, mark_y, cy - 4 + mark_y)
     mark_y = ones_where(iota((cy, nc * cx), 0) == mark_y)
-    for v in every:
-        for n in range(nd):
-            wys[v, pl.ds(n * cz, cz), :] = jnp.where(same_z, given[v][n:n + 1, :], 0.0).astype(bf16)
-        cyt[v] = exact_dot(ay[v], mark_y)
 
     nz = wts.shape[1] // cy
     row_z, col_z = iota((nz, 4 * gz), 0), iota((nz, 4 * gz), 1)
@@ -268,13 +265,32 @@
     tiled = ones_where(lax.rem(iota((8, width), 1), plane4) // cy == iota((8, width), 0))
     low_lane = iota((1, width), 1) >= 2 * plane4
     same_y = lax.rem(iota((cy, width), 1), cy) == iota((cy, width), 0)
-
-    given = [exact_dot(rz[v], pick_z) for v in every]
-    given = [exact_dot(sel_z, given[v]) for v in every]
-    given = [stacked(exact_dot(given[v], tiled), low_lane) for v in every]
+    r8, c8 = iota((8, 8), 0), iota((8, 8), 1)
+
+    def stacked(a, low_lane):
+        high = a.astype(bf16).astype(f32)
+        return jnp.where(low_lane, a - high, high)
+
+    gives_z = [exact_dot(rz[v], pick_z) for v in every]
+    gives_y = [exact_dot(ry[v], pick_y) for v in every]
+    gives_z = [exact_dot(sel_z, gives_z[v]) for v in every]
+    gives_y = [exact_dot(coupled(col_y, block_y, part_y, adv[1, v]), gives_y[v]) for v in every]
+    wide_z = [exact_dot(az[v], spread_z) for v in every]
+    wide_y = [exact_dot(ay[v], spread_y) for v in every]
+    gives_z = [stacked(exact_dot(gives_z[v], tiled), low_lane) for v in every]
+    gives_y = [stacked(exact_dot(gives_y[v], tiled_y), low_y) for v in every]
     for v in every:
+        cyt[v] = exact_dot(ay[v], mark_y)
+        kzh[v], kzl[v] = halves(jnp.where(keep_z, tall(wide_z[v], 8), 0.0))
+        kyh[v], kyl[v] = halves(jnp.where(keep_y, again(wide_y[v], planes), 0.0))
+        high, low = halves(ax[v])
+        axs[v, 0:cx] = jnp.concatenate([high, high], axis=1)
+        axs[v, cx:2 * cx] = jnp.concatenate([low, jnp.zeros_like(low)], axis=1)
+    for v in every:
+        for n in range(nd):
+            wys[v, pl.ds(n * cz, cz), :] = jnp.where(same_z, gives_y[v][n:n + 1, :], 0.0).astype(bf16)
         for n in range(nz):
-            wts[v, pl.ds(n * cy, cy), :] = jnp.where(same_y, given[v][n:n + 1, :], 0.0).astype(bf16)
+            wts[v, pl.ds(n * cy, cy), :] = jnp.where(same_y, gives_z[v][n:n + 1, :], 0.0).astype(bf16)
 
     def part(u, direction):
         ahead = fluxes(u[1], direction)
@@ -364,12 +380,18 @@
     squares = residual(0, 2, squares)
     squares = residual((cz - 2) * cy, 2, squares)
 
-    sub_s = iota((8, cx), 0)
-    tile = jnp.where(sub_s == 5, jnp.max(top, axis=0, keepdims=True), 0.0)
+    lane_s = iota((1, cx), 1)
+    tile = jnp.where(lane_s == nv, jnp.max(top, keepdims=True), 0.0)
     for v in range(nv):
-        tile = jnp.where(sub_s == v, jnp.sum(squares[v], axis=0, keepdims=True), tile)
+        tile = jnp.where(lane_s == v, jnp.sum(squares[v], keepdims=True), tile)
     sty[me[1]] = tile
-    stat_copies = [spread(1, lambda t: sty.at[me[1]], sty.at[me[1]], lambda k: ss.at[0, k], lambda k: sr.at[0, k])]
+    stat_copies = [spread(1, lambda t: sty.at[me[1]], sty.at[me[1]], lambda k: ss.at[k], lambda k: sr.at[k])]
+
+    def gathered(ref, count):
+        result = ref[0]
+        for q in range(1, count):
+            result = jnp.where(lane_s < nv, result + ref[q], jnp.maximum(result, ref[q]))
+        return result
 
     y_copies, z_copies = [], []
 
@@ -413,12 +435,6 @@
         z_copies.append(spread(2, lambda t: zsend.at[v, t], zrecv.at[v, me[2]],
                                lambda k: zs.at[v, k], lambda k: zr.at[v, k]))
 
-    def gathered(ref, count):
-        result = ref[0]
-        for q in range(1, count):
-            result = jnp.where(sub_s < nv, result + ref[q], jnp.maximum(result, ref[q]))
-        return result
-
     for turn in range(nv + 2):
         if turn < nv:
             local_x(turn)
@@ -428,43 +444,70 @@
             local_y(turn)
         if turn >= 2:
             send_z(turn - 2)
+        if turn == 2:
+            for copy in stat_copies[0]:
+                copy.wait_recv()
+            stp[me[2] * gx + me[0]] = gathered(sty, gy)
+            pl.semaphore_wait(joined, gz - 1)
+            mine = stp.at[me[2] * gx + me[0]]
+            stat_copies.append(across(lambda t: mine, mine, ps, pr, True))
         if turn < nv:
             send_y(turn)
 
-    xb[me[0]] = faces_to_rows(lambda v: field[v].reshape(rows, cx))
+    packed = faces_packed(lambda v: field[v].reshape(rows, cx))
+    xb[me[0]] = jnp.transpose(packed)[0:pack]
     x_copies = [spread(0, lambda t: xb.at[me[0]], xb.at[me[0]], lambda k: xs.at[k], lambda k: xr.at[k])]
-    for copy in stat_copies[0]:
-        copy.wait_recv()
-    stx[me[0]] = gathered(sty, gy)
-    stat_copies.append(spread(0, lambda t: stx.at[me[0]], stx.at[me[0]], lambda k: ss.at[1, k], lambda k: sr.at[1, k]))
+
+    def by_variable(table, a, variable):
+        result = None
+        for v in range(nv):
+            term = one_dot(table[v], stack3(jnp.where(variable == v, a, 0.0)))
+            result = term if result is None else result + term
+        return result
+
+    def ends_of(a):
+        return jnp.concatenate([a[0:2 * cy], a[rows - 2 * cy:rows]], axis=0)
+
+    lane_e = iota((plane4, cx), 1)
+    given = by_variable(wts, ends_of(packed), lane_e // 4)
+    eights = 2 * cy // 8
+    for t in range(gz):
+        piece = given[t * 2 * cy:t * 2 * cy + 8]
+        for j in range(1, eights):
+            piece = piece + pltpu.roll(given[t * 2 * cy + 8 * j:t * 2 * cy + 8 * j + 8], 32 * j, 1)
+        esend[t] = piece
+    e_copies = across(lambda t: esend.at[t], erecv.at[me[2] * gx + me[0]], es, er, False)
 
     mb[...] = jnp.zeros_like(mb)
+    mw[...] = jnp.zeros_like(mw)
     cxf[...] = jnp.zeros_like(cxf)
     wide_x = gx * pack
-    in_x = lax.rem(iota((4 * gx, wide_x), 1), pack)
-    block_x = iota((4 * gx, wide_x), 1) // pack
     row_x = iota((8, 4 * gx), 0)
-    placed = [exact_dot(coupled(iota((8, 4 * gx), 1), me[0], row_x, adv[0, v]), rx[v]) for v in every]
-    to_pack = [ones_where((in_x // 4 == v) & (iota((4 * gx, wide_x), 0) == 4 * block_x + lax.rem(in_x + 2, 4)))
-               for v in every]
-    placed = [exact_dot(placed[v], to_pack[v]) for v in every]
+    row_l, col_l = iota((8, 4 * gz), 0), iota((8, 4 * gz), 1)
+    sel_lf = ones_where((row_l < 4) & (col_l == 4 * me[2] + jnp.where(row_l < 2, row_l - 2, row_l + 2)))
+    near = [exact_dot(sel_lf, rz[v]) for v in every]
+    columns_z = [exact_dot(az[v], face_pick((8, cz), cz), NT) for v in every]
+    terms = [exact_dot(coupled(iota((8, 4 * gx), 1), me[0], row_x, adv[0, v]), rx[v]) for v in every]
+
+    def to_pack(v, pitch):
+        spot = lax.rem(iota((4 * gx, gx * pitch), 1), pitch)
+        block = iota((4 * gx, gx * pitch), 1) // pitch
+        return ones_where((spot // 4 == v) & (iota((4 * gx, gx * pitch), 0) == 4 * block + lax.rem(spot + 2, 4)))
+
+    square = [exact_dot(near[v], sel_lf, NT) for v in every]
+    own = [exact_dot(near[v], pick_z) for v in every]
+    placed = [exact_dot(terms[v], to_pack(v, pack)) for v in every]
+    wider = [exact_dot(terms[v], to_pack(v, 32)) for v in every]
     columns = [exact_dot(face_pick((8, cx), cx), ax[v], NT) for v in every]
     for v in every:
         high = columns[v].astype(bf16).astype(f32)
         for k in range(3):
             at = pl.ds(4 * v + 32 * k, 4)
             mb[at, :] = placed[v][0:4]
+            mw[at, :] = wider[v][0:4]
             cxf[at, v * cx:(v + 1) * cx] = (high if k < 2 else columns[v] - high)[0:4]
 
     cxb[...] = cxf[...].astype(bf16)
-
-    row_l, col_l = iota((8, 4 * gz), 0), iota((8, 4 * gz), 1)
-    sel_lf = ones_where((row_l < 4) & (col_l == 4 * me[2] + jnp.where(row_l < 2, row_l - 2, row_l + 2)))
-    r8, c8 = iota((8, 8), 0), iota((8, 8), 1)
-    near = [exact_dot(sel_lf, rz[v]) for v in every]
-    square = [exact_dot(near[v], sel_lf, NT) for v in every]
-    own = [exact_dot(near[v], pick_z) for v in every]
-    columns = [exact_dot(az[v], face_pick((8, cz), cz), NT) for v in every]
 
     def mixed(v):
         def e(i, j):
@@ -494,8 +537,8 @@
     peers = [exact_dot(weighed(v), mixed(v)) for v in every]
     own = [exact_dot(own[v], tiled) for v in every]
     peers = [exact_dot(peers[v], tiled) for v in every]
-    own = [stacked(exact_dot(columns[v], own[v]), low_lane) for v in every]
-    peers = [stacked(exact_dot(columns[v], peers[v]), low_lane) for v in every]
+    own = [stacked(exact_dot(columns_z[v], own[v]), low_lane) for v in every]
+    peers = [stacked(exact_dot(columns_z[v], peers[v]), low_lane) for v in every]
     for v in every:
         for z in range(cz):
             pto[v, pl.ds(z * cy, cy), :] = jnp.where(same_y, own[v][z:z + 1, :], 0.0).astype(bf16)
@@ -504,27 +547,11 @@
     for v in every:
         field[v] = field[v] - one_dot(pto[v], stack3(end_planes(v))).reshape(cz, cy, cx)
 
-    for group in x_copies + [stat_copies[1]]:
-        for copy in group:
-            copy.wait_recv()
-    stz[me[2]] = gathered(stx, gx)
-    stat_copies.append(spread(2, lambda t: stz.at[me[2]], stz.at[me[2]], lambda k: ss.at[2, k], lambda k: sr.at[2, k]))
-
+    for copy in x_copies[0]:
+        copy.wait_recv()
     ext[...] = jnp.transpose(split_dot(halves(mb[...]), halves(xb[...].reshape(wide_x, rows))))
-    lane_e = iota((plane4, cx), 1)
     lane_v = jnp.where(lane_e < 96, (lane_e % 32) // 4, -1)
-    ends = jnp.concatenate([ext[pl.ds(0, 2 * cy), :], ext[pl.ds((cz - 2) * cy, 2 * cy), :]], axis=0)
-
-    def by_variable(table, a):
-        result = None
-        for v in range(nv):
-            term = one_dot(table[v], stack3(jnp.where(lane_v == v, a, 0.0)))
-            result = term if result is None else result + term
-        return result
-
-    esend[...] = by_variable(wts, ends)[0:gz * 2 * cy].reshape(gz, 2 * cy, cx)
-    e_copies = spread(2, lambda t: esend.at[t], erecv.at[me[2]], lambda k: es.at[k], lambda k: er.at[k])
-    ext[...] = ext[...] - by_variable(pto, ends)
+    ext[...] = ext[...] - by_variable(pto, ends_of(ext), lane_v)
 
     def sides(load):
         before, after = None, None
@@ -544,20 +571,35 @@
     for v in every:
         field[v] = field[v] - one_dot(parts, cxb[:, v * cx:(v + 1) * cx]).reshape(cz, cy, cx)
 
-    for copy in stat_copies[2]:
+    for copy in stat_copies[1]:
         copy.wait_recv()
-    final = gathered(stz, gz)
-    norm = jnp.sqrt(jnp.sum(final, axis=1, keepdims=True) / float(cells))
-    fastest = courant / jnp.max(final, axis=1, keepdims=True)
-    stats_out[...] = jnp.broadcast_to(norm, (8, cx))
-    time_step = fastest[5:6, :]
+    final = gathered(stp, gz * gx)
+    stats_out[...] = jnp.broadcast_to(jnp.sqrt(final / float(cells)), (8, cx))
+    time_step = courant / final[:, nv:nv + 1]
 
     for copy in e_copies:
         copy.wait_recv()
     for v in every:
         for copy in z_copies[v]:
             copy.wait_recv()
-    parts = doubled(sides(lambda q: erecv[q]), lane_e)
+    lane_8 = iota((8, cx), 1)
+    sums = [[None] * gx, [None] * gx]
+    for p in range(gx):
+        for k in range(1, gz):
+            q = lax.rem(me[2] + k, gz)
+            value = erecv[q * gx + p]
+            for side, term in enumerate([jnp.where(q < me[2], value, 0.0), jnp.where(q > me[2], value, 0.0)]):
+                sums[side][p] = term if k == 1 else sums[side][p] + term
+    pieces = []
+    for side in range(2):
+        for j in range(eights):
+            piece = jnp.zeros((8, cx), f32)
+            for p in range(gx):
+                turned = (32 * (p - j)) % cx
+                moved = sums[side][p] if turned == 0 else pltpu.roll(sums[side][p], turned, 1)
+                piece = jnp.where(lane_8 // 32 == p, moved, piece)
+            pieces.append(piece)
+    parts = doubled(split_dot(halves(jnp.concatenate(pieces, axis=0)), halves(mw[...]), NT), lane_e)
     shares = [sides(lambda q: zrecv[v, q]) - one_dot(parts, cxb[:, v * cx:(v + 1) * cx]) for v in every]
     for v in every:
         out[v] = (field[v].reshape(rows, cx) - one_dot(pts[v], stack3(shares[v]))) * time_step
@@ -574,7 +616,7 @@
         copy.start()
         copies.append(copy)
     for v in range(nv):
-        norm[v] = stats[v, 0]
+        norm[v] = stats[0, v]
     for copy in copies:
         copy.wait()
 
@@ -584,7 +626,6 @@
     gx, gy, gz = counts
     rows = cz * cy
     cells = rows * cx * gx * gy * gz
-    most = max(counts) - 1
     hbm = pl.BlockSpec(memory_space=pltpu.HBM)
     vmem = pl.BlockSpec(memory_space=pltpu.VMEM)
     dma = pltpu.SemaphoreType.DMA
@@ -621,6 +662,7 @@
             pltpu.VMEM((nv, 2 * cx, 2 * cx), bf16),
             pltpu.VMEM((nv, cy, nc * cx), f32),
             pltpu.VMEM((cx, gx * pack), f32),
+            pltpu.VMEM((cx, gx * 32), f32),
             pltpu.VMEM((cx, nv * cx), f32),
             pltpu.VMEM((cx, nv * cx), bf16),
             pltpu.VMEM((gx, pack, rows), f32),
@@ -628,11 +670,10 @@
             pltpu.VMEM((nv, gy, nc * cz, cx), f32),
             pltpu.VMEM((nv, gz, 2 * cy, cx), f32),
             pltpu.VMEM((nv, gz, 2 * cy, cx), f32),
-            pltpu.VMEM((gz, 2 * cy, cx), f32),
-            pltpu.VMEM((gz, 2 * cy, cx), f32),
-            pltpu.VMEM((gx, 8, cx), f32),
-            pltpu.VMEM((gy, 8, cx), f32),
             pltpu.VMEM((gz, 8, cx), f32),
+            pltpu.VMEM((gz * gx, 8, cx), f32),
+            pltpu.VMEM((gz * gx, 1, cx), f32),
+            pltpu.VMEM((gy, 1, cx), f32),
             pltpu.VMEM(inverse_x.shape, f32),
             pltpu.VMEM(inverse_y.shape, f32),
             pltpu.VMEM(inverse_z.shape, f32),
@@ -646,8 +687,10 @@
             dma((gx - 1,)), dma((gx - 1,)),
             dma((nv, gy - 1)), dma((nv, gy - 1)),
             dma((nv, gz - 1)), dma((nv, gz - 1)),
-            dma((gz - 1,)), dma((gz - 1,)),
-            dma((3, most)), dma((3, most)),
+            dma((gz * gx,)), dma((gz * gx,)),
+            dma((gz * gx,)), dma((gz * gx,)),
+            dma((gy - 1,)), dma((gy - 1,)),
+            pltpu.SemaphoreType.REGULAR,
         ],
         compiler_params=pltpu.CompilerParams(
             collective_id=0, has_side_effects=True, vmem_limit_bytes=60 * 1024 * 1024),

time: 31.6 us -> 30.5 us (0.965)
  Pallas kernels: 30.8 us -> 29.7 us
    pallas_call x1, Pallas kernels: 29.2 us -> 28.1 us  [shards(): pl.pallas_call(functools.partial(kernel, (counts, nv, cz, cy, cx, cells))...]
where the time goes in v4:
time: 30.5 us; the launch traced here: 30.3 us
  Pallas kernels  29.7 us (97%)
  between operations  0.64 us (2%)
    pallas_call x1, Pallas kernels, shards(): pl.pallas_call(functools.partial(kernel, (counts, nv, cz, cy, cx, cells))...  28.1 us
    pallas_call x1, Pallas kernels, shards(): pl.pallas_call(functools.partial(finish, nv), out_shape=(jax.ShapeDtypeSt...  1.61 us

profile of v4, /device:TPU:0, one launch (start us, length us, event | category | flops | bytes accessed | tf_op | source)
XLA Modules:
  0.0 30.3 jit_solution(5898138912026439176)
XLA Ops:
  0.6 28.1 %shard_map.95 = (f32[5,512,128]{2,1,0:T(8,128)S(1)}, f32[8,128]{1,0:T(8,128)S(1)}) custom-call(f32[5,512,128]{2,1,0:T(8,128)} %bitcast.2, f32[3,5]{1,0:T(4,128)} %adv_h.1, f32[5,128,128]{2,1,0:T(8,128)} %ax_h.1, f32[5,16,16]{2,1,0:T(8,128)} %ay_h.1, f32[5,32,32]{2,1,0:T(8,128)} %az_h.1, f32[5,16,16]{2,1,0:T(8,128)} %rx_h.1, f32[5,8,8]{2,1,0:T(8,128)} %ry_h.1, ...), custom_call_target="tpu_custom_call" | custom-call | tf_op jit(solution)/shard_map/pallas_call | solution.py:638
  28.7 1.6 %shard_map.96 = (f32[5,512,128]{2,1,0:T(8,128)}, f32[5]{0:T(128)}) custom-call(f32[5,512,128]{2,1,0:T(8,128)S(1)} %get-tuple-element.6.solved, f32[8,128]{1,0:T(8,128)S(1)} %get-tuple-element.7.stats), custom_call_target="tpu_custom_call" | custom-call | tf_op jit(solution)/shard_map/pallas_call | solution.py:698

commit v5 on v4

--- a/solution.py
+++ b/solution.py
@@ -338,14 +338,14 @@
         parts = jnp.concatenate([high, mid, both - high - mid, jnp.zeros_like(both)], axis=0).astype(bf16)
         edge[v] = one_dot(parts, weights, TN)
 
-    def residual(base, planes, squares):
+    def residual(base, planes, squares, which=None):
         size = planes * cy
         here = pl.ds(base + 2 * cy, size)
         vx, pc = vel[0, here, :], prs[here, :]
         around = pl.ds(base + cy, size + 2 * cy)
         vz, pz = vel[2, around, :], prs[around, :]
         found = []
-        for v in range(nv):
+        for i, v in enumerate(range(nv) if which is None else [which]):
             u = uz[v, pl.ds(base, size + 4 * cy), :]
             inner = u[cy:size + 3 * cy]
             c = u[2 * cy:size + 2 * cy]
@@ -365,14 +365,17 @@
             at = pl.ds(base, size)
             value = (res[v, at, :] + edge[v, at, :]) + (along_z + along_x) - 12.0 * damping * c
             res[v, at, :] = value
-            found.append(squares[v] + jnp.sum((value * value).reshape(planes, cy, cx), axis=0))
+            found.append(squares[i] + jnp.sum((value * value).reshape(planes, cy, cx), axis=0))
         return tuple(found)
 
     planes_in = next(n for n in (7, 4, 2, 1) if (cz - 4) % n == 0)
-    squares = lax.fori_loop(
-        0, (cz - 4) // planes_in,
-        lambda i, c: residual(pl.multiple_of(2 * cy + i * planes_in * cy, 8), planes_in, c),
-        (jnp.zeros((cy, cx), f32),) * nv)
+    planes_in = next(n for n in (28, 4, 2, 1) if (cz - 4) % n == 0)
+    squares = []
+    for v in every:
+        squares += lax.fori_loop(
+            0, (cz - 4) // planes_in,
+            lambda i, c: residual(pl.multiple_of(2 * cy + i * planes_in * cy, 8), planes_in, c, v),
+            (jnp.zeros((cy, cx), f32),))
     for copy in z_halo:
         copy.wait_recv()
     derive(0, 2 * cy)

time: 30.5 us -> 30.4 us (level)
  no operation moved by 1% of the time
where the time goes in v5:
time: 30.4 us; the launch traced here: 30.2 us
  Pallas kernels  29.6 us (97%)
  between operations  0.64 us (2%)
    pallas_call x1, Pallas kernels, shards(): pl.pallas_call(functools.partial(kernel, (counts, nv, cz, cy, cx, cells))...  28 us
    pallas_call x1, Pallas kernels, shards(): pl.pallas_call(functools.partial(finish, nv), out_shape=(jax.ShapeDtypeSt...  1.61 us

profile of v5, /device:TPU:0, one launch (start us, length us, event | category | flops | bytes accessed | tf_op | source)
XLA Modules:
  0.0 30.2 jit_solution(1258107591558968791)
XLA Ops:
  0.6 28.0 %shard_map.95 = (f32[5,512,128]{2,1,0:T(8,128)S(1)}, f32[8,128]{1,0:T(8,128)S(1)}) custom-call(f32[5,512,128]{2,1,0:T(8,128)} %bitcast.2, f32[3,5]{1,0:T(4,128)} %adv_h.1, f32[5,128,128]{2,1,0:T(8,128)} %ax_h.1, f32[5,16,16]{2,1,0:T(8,128)} %ay_h.1, f32[5,32,32]{2,1,0:T(8,128)} %az_h.1, f32[5,16,16]{2,1,0:T(8,128)} %rx_h.1, f32[5,8,8]{2,1,0:T(8,128)} %ry_h.1, ...), custom_call_target="tpu_custom_call" | custom-call | tf_op jit(solution)/shard_map/pallas_call | solution.py:641
  28.6 1.6 %shard_map.96 = (f32[5,512,128]{2,1,0:T(8,128)}, f32[5]{0:T(128)}) custom-call(f32[5,512,128]{2,1,0:T(8,128)S(1)} %get-tuple-element.6.solved, f32[8,128]{1,0:T(8,128)S(1)} %get-tuple-element.7.stats), custom_call_target="tpu_custom_call" | custom-call | tf_op jit(solution)/shard_map/pallas_call | solution.py:701
